TPU v7x, 256 devices: a 8x8x2 block of a 8x8x16 slice. The times are simulated.
256 devices in a mesh: groups: 2 (over z), seq: 16 (over x, core), qset: 8 (over y).
Axes of the slice: x: 8, y: 8, z: 2, core: 2. Of those that a mesh axis runs over, the one named last changes fastest.
The devices are a block of a 8x8x16 slice.
Arguments:
- states: bfloat16 [16, 16, 128, 4096], P(('groups', 'qset'), 'seq'), parts along dimension 0, may hold values from -7 to 7
- enc_gain: bfloat16 [4096], replicated, may hold values from 0.25 to 1.75
- dec_states: bfloat16 [32, 64, 4096], P(('groups', 'qset')), parts along dimension 0, may hold values from -7 to 7
- dec_gain: bfloat16 [4096], replicated, may hold values from 0.25 to 1.75
- query_weight: bfloat16 [4096, 4096], P(None, 'seq'), may hold values from -0.375 to 0.375
- key_value_weight: bfloat16 [4096, 2, 4096], P(None, None, 'seq'), may hold values from -0.0625 to 0.0625
- out_weight: bfloat16 [4096, 4096], P('seq'), may hold values from -0.75 to 0.75
- question_of: int32 [16, 16, 1], P('groups'), parts along dimension 0, may hold values from 0 to 15; in each aligned block of 16 rows (0 to 15, 16 to 31, ..., all dimensions but the last counted through in order) at most 2 rows name the same one
Outputs:
- mixed: bfloat16 [32, 64, 4096], P(('groups', 'qset'), None, 'seq'), parts along dimension 0
There are 2 independent parts, one for each index of `groups`. A program takes and returns all parts, laid end to end along the dimension named above; an argument that names none is the same for every part. Nothing has to cross between parts.
Inputs may be any that keep to these rules, and one draw needn't show every extreme that they name: `question_of`: within each index of the first dimension (one source group of 16 passages) at most 2 passages name the same question, and exactly 2 do for some question in some groups; every question is named by at least one passage.
All inputs are finite; a program needn't handle non-finite values.
Results may differ from a plain program's by a relative error of at most 0.014.
The roundings to bfloat16 on the way count: a program that leaves them out, or rounds other values in their place, can miss the bound.
Values may be sent and summed in bfloat16 or wider, within the bound.
A program may use at most 128 MiB of HBM per device.

v0:
```python
import math

import jax
import jax.numpy as jnp
from jax import lax
from jax.sharding import PartitionSpec as P

HD = 64
CAP = 2


EPSILON = 1e-06
MASKED_SCORE = -1e30


def from_everyone(shard, axis):
    devices = lax.axis_size(axis)
    return lax.all_to_all(
        jnp.broadcast_to(shard[None], (devices, *shard.shape)), axis, 0, 0, tiled=True
    )


def laid_out(pieces, dim):
    dims = list(pieces.shape[1:])
    dims[dim] *= pieces.shape[0]
    return jnp.moveaxis(pieces, 0, dim).reshape(dims)


def gather_directly(shard, axis, dim):
    pieces = from_everyone(shard, axis)
    return laid_out(pieces, dim)


def over_copies(shard, axis):
    return from_everyone(shard, axis).max(axis=0)


def split_up(shard, dim, devices):
    dims = shard.shape
    pieces = shard.reshape(*dims[:dim], devices, dims[dim] // devices, *dims[dim + 1 :])
    return jnp.moveaxis(pieces, dim, 0)


def sent_and_summed(shard, axis, dim):
    pieces = split_up(shard, dim, lax.axis_size(axis))
    arrived = lax.all_to_all(pieces, axis, split_axis=0, concat_axis=0, tiled=True)
    return arrived.astype(jnp.float32).sum(axis=0)


def sent_together(arrays, axis, dim, along):
    widths = [math.prod(a.shape[along:]) for a in arrays]
    both = jnp.concatenate(
        [a.reshape(*a.shape[:along], w) for a, w in zip(arrays, widths)], axis=along
    )
    result = sent_and_summed(both, axis, dim)
    pieces = jnp.split(result, [sum(widths[:k]) for k in range(1, len(widths))], axis=along)
    return tuple(
        (b.reshape(*result.shape[:along], *a.shape[along:]) for a, b in zip(arrays, pieces))
    )


def scaled_norm(rows_in, gain_vec):
    rows_f32 = rows_in.astype(jnp.float32)
    mean_square = jnp.mean(rows_f32 * rows_f32, axis=-1, keepdims=True)
    return rows_f32 * lax.rsqrt(mean_square + EPSILON) * gain_vec.astype(jnp.float32)


def body(
    states, enc_gain, dec_states, dec_gain, query_weight, key_value_weight, out_weight, question_of
):
    model_width = states.shape[-1]
    passage_len = states.shape[2]
    group_count = lax.axis_size("qset")
    shard_count = lax.axis_size("seq")
    group_index = lax.axis_index("qset")
    shard_index = lax.axis_index("seq")
    local_questions = dec_states.shape[0]
    dec_len = dec_states.shape[1]
    head_cols = query_weight.shape[1]
    heads_here = head_cols // HD
    all_questions = local_questions * group_count
    kv_weight = key_value_weight.reshape(model_width, 2 * head_cols)
    own_rows = scaled_norm(states[0, 0], enc_gain).astype(jnp.bfloat16)[None]
    gathered_rows = lax.all_gather(own_rows, "seq", axis=0, tiled=True)
    piece_count = gathered_rows.shape[0]
    flat_rows = gathered_rows.reshape(piece_count * passage_len, model_width)
    product = jnp.dot(flat_rows, kv_weight, preferred_element_type=jnp.float32)
    key_vals = product.astype(jnp.bfloat16).reshape(piece_count, passage_len, 2 * head_cols)
    passage_table = question_of[:, :, 0]
    numbers = jnp.arange(all_questions, dtype=jnp.int32)
    counts = jnp.sum(
        (passage_table[:, :, None] == numbers[None, None, :]).astype(jnp.int32), axis=1
    )
    group_table = lax.dynamic_index_in_dim(passage_table, group_index, 0, keepdims=False)
    matches = (group_table[:, None] == numbers[None, :]).astype(jnp.int32)
    earlier = jnp.cumsum(matches, axis=0) - matches
    slot_rank = jnp.sum(earlier * matches, axis=1)
    slot_index = group_table * CAP + slot_rank
    picker = (
        jnp.arange(all_questions * CAP, dtype=jnp.int32)[:, None] == slot_index[None, :]
    ).astype(jnp.bfloat16)
    packed = jnp.einsum("as,spc->apc", picker, key_vals, preferred_element_type=jnp.float32).astype(
        jnp.bfloat16
    )
    dec_rows = (
        scaled_norm(dec_states, dec_gain)
        .astype(jnp.bfloat16)
        .reshape(local_questions * dec_len, model_width)
    )
    queries = jnp.dot(dec_rows, query_weight, preferred_element_type=jnp.float32)
    queries = queries.astype(jnp.bfloat16).reshape(local_questions, dec_len, heads_here, HD)
    slot_numbers = jnp.arange(CAP, dtype=jnp.int32)
    gathered = gather_directly(queries, "qset", 0)
    local_keys = packed.reshape(all_questions, CAP * passage_len, 2 * head_cols)
    key_rows = local_keys[:, :, :head_cols].reshape(all_questions, -1, heads_here, HD)
    value_rows = local_keys[:, :, head_cols:].reshape(all_questions, -1, heads_here, HD)
    own_counts = lax.dynamic_index_in_dim(counts, group_index, 0, keepdims=False)
    live_slots = own_counts[:, None] > slot_numbers[None, :]
    live_rows = jnp.broadcast_to(live_slots[:, :, None], (all_questions, CAP, passage_len)).reshape(
        all_questions, -1
    )
    scores = jnp.einsum("qthd,qrhd->qhtr", gathered, key_rows, preferred_element_type=jnp.float32)
    scores = jnp.where(live_rows[:, None, None, :], scores, MASKED_SCORE)
    row_peak = over_copies(jnp.max(scores, axis=-1), "qset")
    weights = jnp.where(live_rows[:, None, None, :], jnp.exp(scores - row_peak[..., None]), 0.0)
    group_total = jnp.sum(weights, axis=-1)
    group_summed = jnp.einsum(
        "qhtr,qrhd->qthd",
        weights.astype(jnp.bfloat16),
        value_rows,
        preferred_element_type=jnp.float32,
    )
    summed, row_total = sent_together(
        (group_summed.astype(jnp.bfloat16), group_total.astype(jnp.bfloat16)), "qset", 0, 1
    )
    attended = summed / jnp.transpose(row_total, (0, 2, 1))[..., None]
    attended = attended.astype(jnp.bfloat16).reshape(local_questions * dec_len, head_cols)
    piece_cols = model_width // shard_count
    residual = lax.dynamic_slice_in_dim(dec_states, shard_index * piece_cols, piece_cols, 2).astype(
        jnp.float32
    )
    owned_rows = sent_and_summed(
        lax.dot_general(
            out_weight, attended, (((0,), (1,)), ((), ())), preferred_element_type=jnp.float32
        ).astype(jnp.bfloat16),
        "seq",
        0,
    )
    owned_sum = jnp.transpose(owned_rows).reshape(local_questions, dec_len, piece_cols)
    return (residual + owned_sum).astype(jnp.bfloat16)


def solution(mesh):
    return jax.shard_map(
        body,
        mesh=mesh,
        in_specs=(
            P(("groups", "qset"), "seq", None, None),
            P(),
            P(("groups", "qset"), None, None),
            P(),
            P(None, "seq"),
            P(None, None, "seq"),
            P("seq", None),
            P("groups", None, None),
        ),
        out_specs=P(("groups", "qset"), None, "seq"),
        check_vma=False,
    )
```

profile of v0, /device:TPU:513, one launch (start us, length us, event | category | flops | bytes accessed | tf_op | source)
XLA Modules:
  0.0 255.8 jit_solution(8536282614529816746)
XLA Ops:
  7.4 1.6 fusion.8
  9.0 2.6 %fusion.7 = bf16[1,128,4096]{2,1,0:T(8,128)(2,1)} fusion(bf16[1,1,128,4096]{3,2,1,0:T(8,128)(2,1)} %param.8, f32[4096]{0:T(1024)S(1)} %convert_element_type.98, f32[128]{0:T(128)S(1)} %add_rsqrt_fusion.1), kind=kLoop, calls=%fused_computation.16 | loop fusion | flops 2097152 | bytes 2114048 | tf_op jit(solution)/shard_map/convert_element_type | solution.py:83
  12.3 0.9 copy-done.3
  13.9 1.2 broadcast_bitcast_fusion
  15.1 3.0 %reshape.185 = bf16[8,2,16384]{2,1,0:T(2,128)(2,1)} reshape(bf16[8,2,4,64,64]{4,3,2,1,0:T(8,128)(2,1)} %broadcast_bitcast_fusion) | data formatting | bytes 1048576
  18.1 13.7 %all-to-all-start = ((bf16[8,2,16384]{2,1,0:T(2,128)(2,1)}), bf16[8,2,16384]{2,1,0:T(2,128)(2,1)}, u32[]{:S(2)}, u32[]{:S(2)}) async-start(bf16[8,2,16384]{2,1,0:T(2,128)(2,1)} %reshape.185), calls=%async_computation | async-start | bytes 1048576 | tf_op jit(solution)/shard_map/all_to_all | solution.py:18
  31.9 4.8 %copy.47 = bf16[512,8,2,256]{3,1,2,0:T(8,128)(2,1)} copy(bf16[512,8,2,256]{3,2,1,0:T(2,128)(2,1)} %bitcast.61) | data formatting | bytes 8388608
  37.3 6.8 %all-to-all-done = bf16[8,2,16384]{2,1,0:T(2,128)(2,1)} async-done(((bf16[8,2,16384]{2,1,0:T(2,128)(2,1)}), bf16[8,2,16384]{2,1,0:T(2,128)(2,1)}, u32[]{:S(2)}, u32[]{:S(2)}) %all-to-all-start) | async-done | bytes 524320 | tf_op jit(solution)/shard_map/all_to_all | solution.py:18
  44.1 3.1 %reshape.186 = bf16[8,2,4,64,64]{4,3,2,1,0:T(8,128)(2,1)} reshape(bf16[8,2,16384]{2,1,0:T(2,128)(2,1)} %all-to-all-done) | data formatting | bytes 1048576
  47.1 80.0 %all-gather.2.cloned.1.call-done = bf16[16,128,4096]{2,1,0:T(8,128)(2,1)} async-done(((bf16[1,128,4096]{2,1,0:T(8,128)(2,1)}), bf16[16,128,4096]{2,1,0:T(8,128)(2,1)}) %all-gather.2.cloned.1.call-update) | async-done | bytes 16777232 | tf_op jit(solution)/shard_map/all_gather | solution.py:84
  127.2 13.6 %convolution_convert_fusion.1 = bf16[2048,512]{1,0:T(8,128)(2,1)S(1)} fusion(bf16[2048,4096]{1,0:T(8,128)(2,1)} %bitcast.74, bf16[4096,512]{1,0:T(8,128)(2,1)} %bitcast.62), kind=kOutput, calls=%fused_computation.5 | convolution fusion | flops 8590983168 | bytes 23068672 | tf_op jit(solution)/shard_map/dot_general | solution.py:87
  140.8 1.6 convolution_convert_fusion.2
  142.4 2.4 copy.37
  144.8 2.5 fusion.30
  147.3 3.9 %copy.40 = bf16[16,256,256]{1,2,0:T(8,128)(2,1)} copy(bf16[16,256,256]{2,1,0:T(8,128)(2,1)} %get-tuple-element.6) | data formatting | bytes 4194304 | tf_op jit(solution)/shard_map/slice | solution.py:115
  151.2 4.5 %select_reduce_fusion = (f32[16,4,64]{2,1,0:T(4,128)S(1)}, f32[16,4,64,256]{3,2,1,0:T(8,128)}) fusion(pred[16,256]{1,0:T(8,128)(4,1)S(1)} %bitcast.68, bf16[16,64,4,64]{3,1,2,0:T(8,128)(2,1)} %bitcast.59, bf16[16,256,4,64]{1,3,2,0:T(8,128)(2,1)} %bitcast.58), kind=kOutput, calls=%fused_computation.2 | convolution fusion | flops 136310784 | bytes 6836224 | tf_op jit(solution)/shard_map/qthd,qrhd->qhtr/dot_general | solution.py:122
  156.6 6.7 %all-to-all-start.1 = ((f32[8,1,4096]{2,1,0:T(1,128)}), f32[8,1,4096]{2,1,0:T(1,128)S(1)}, u32[]{:S(2)}, u32[]{:S(2)}) async-start(f32[8,1,4096]{2,1,0:T(1,128)} %reshape.187), calls=%async_computation.1 | async-start | bytes 262144 | tf_op jit(solution)/shard_map/all_to_all | solution.py:18
  163.3 3.9 %copy.38 = bf16[16,256,256]{1,2,0:T(8,128)(2,1)} copy(bf16[16,256,256]{2,1,0:T(8,128)(2,1)} %get-tuple-element.5) | data formatting | bytes 4194304 | tf_op jit(solution)/shard_map/slice | solution.py:116
  167.2 4.2 %all-to-all-done.1 = f32[8,1,4096]{2,1,0:T(1,128)S(1)} async-done(((f32[8,1,4096]{2,1,0:T(1,128)}), f32[8,1,4096]{2,1,0:T(1,128)S(1)}, u32[]{:S(2)}, u32[]{:S(2)}) %all-to-all-start.1) | async-done | bytes 131104 | tf_op jit(solution)/shard_map/all_to_all | solution.py:18
  172.0 1.0 reduce.1
  173.1 3.3 %fusion = bf16[16,4,64]{2,1,0:T(4,128)(2,1)S(1)} fusion(f32[16,4,64,256]{3,2,1,0:T(8,128)} %get-tuple-element.8, f32[16,4,64]{2,1,0:T(4,128)S(1)} %copy.42, pred[16,256]{1,0:T(8,128)(4,1)S(1)} %bitcast.69), kind=kLoop, calls=%fused_computation.3 | loop fusion | flops 4190208 | bytes 4222976 | tf_op jit(solution)/shard_map/reduce_sum | solution.py:126
  176.5 3.5 %fusion.19 = bf16[16,64,4,64]{1,3,2,0:T(8,128)(2,1)} fusion(bf16[16,256,4,64]{1,3,2,0:T(8,128)(2,1)} %bitcast.66, f32[16,4,64,256]{3,2,1,0:T(8,128)S(1)} %copy-done.1, f32[16,4,64]{2,1,0:T(4,128)S(1)} %copy.42, pred[16,256]{1,0:T(8,128)(4,1)S(1)} %bitcast.70), kind=kOutput, calls=%fused_computation.26 | convolution fusion | flops 138674176 | bytes 6836224 | tf_op jit(solution)/shard_map/qhtr,qrhd->qthd/dot_general | solution.py:127
  180.0 2.4 copy.43
  182.4 3.3 %concatenate.6 = bf16[8,2,16384]{2,1,0:T(2,128)(2,1)} reshape(bf16[16,64,4,64]{3,2,1,0:T(4,128)(2,1)} %copy.43) | data formatting | bytes 1048576 | tf_op jit(solution)/shard_map/concatenate | solution.py:52
  185.9 1.5 pad_maximum_fusion
  187.4 17.2 %all_to_all.20 = bf16[8,2,16640]{2,1,0:T(2,128)(2,1)S(1)} all-to-all(bf16[8,2,16640]{2,1,0:T(2,128)(2,1)S(1)} %pad_maximum_fusion), channel_id=1, replica_groups=mesh['groups'=2,'seq'=16,'qset'=8] {'qset'}, dimensions={0} | all-to-all | bytes 1064960 | tf_op jit(solution)/shard_map/all_to_all | solution.py:46
  206.0 1.0 div.27
  208.0 1.4 convolution_convert_fusion
  209.3 1.1 copy.53
  210.5 8.4 %all-to-all-start.3 = ((bf16[16,256,128]{1,2,0:T(8,128)(2,1)}), bf16[16,256,128]{1,2,0:T(8,128)(2,1)}, u32[]{:S(2)}, u32[]{:S(2)}) async-start(bf16[16,256,128]{1,2,0:T(8,128)(2,1)} %bitcast.63), calls=%async_computation.3 | async-start | bytes 2097152 | tf_op jit(solution)/shard_map/all_to_all | solution.py:46
  218.8 28.1 %all-to-all-done.3 = bf16[16,256,128]{1,2,0:T(8,128)(2,1)} async-done(((bf16[16,256,128]{1,2,0:T(8,128)(2,1)}), bf16[16,256,128]{1,2,0:T(8,128)(2,1)}, u32[]{:S(2)}, u32[]{:S(2)}) %all-to-all-start.3) | async-done | bytes 1048608 | tf_op jit(solution)/shard_map/all_to_all | solution.py:46
  246.9 1.4 convert_reduce_fusion
  (48 shorter events, 7.4 us)
Async XLA Ops:
  6.5 201.4 %copy-start = (bf16[256,4096]{1,0:T(8,128)(2,1)S(1)}, bf16[256,4096]{1,0:T(8,128)(2,1)}, u32[]{:S(2)}) copy-start(bf16[256,4096]{1,0:T(8,128)(2,1)} %param.14) | copy-start | bytes 6291460
  6.6 120.6 %all-gather.2.cloned.1.call-start = ((), (), s32[]{:S(2)}) async-start(), calls=%async_computation.4 | async-start | bytes 17825792 | tf_op jit(solution)/shard_map/all_gather | solution.py:84
  7.4 4.3 %copy-start.4 = (bf16[4096]{0:T(1024)(128)(2,1)S(1)}, bf16[4096]{0:T(1024)(128)(2,1)}, u32[]{:S(2)}) copy-start(bf16[4096]{0:T(1024)(128)(2,1)} %param.11) | copy-start | bytes 24580
  7.4 4.3 %copy-start.2 = (bf16[2,64,4096]{2,1,0:T(8,128)(2,1)S(1)}, bf16[2,64,4096]{2,1,0:T(8,128)(2,1)}, u32[]{:S(2)}) copy-start(bf16[2,64,4096]{2,1,0:T(8,128)(2,1)} %param.10) | copy-start | bytes 3145732
  11.7 1.6 copy-start.3
  13.7 18.1 %copy-start.5 = (s32[8,16,1]{1,2,0:T(1,128)S(1)}, s32[8,16,1]{1,2,0:T(1,128)}, u32[]{:S(2)}) copy-start(s32[8,16,1]{1,2,0:T(1,128)} %param.15) | copy-start | bytes 1540
  18.1 25.9 %all-to-all-start = ((bf16[8,2,16384]{2,1,0:T(2,128)(2,1)}), bf16[8,2,16384]{2,1,0:T(2,128)(2,1)}, u32[]{:S(2)}, u32[]{:S(2)}) async-start(bf16[8,2,16384]{2,1,0:T(2,128)(2,1)} %reshape.185), calls=%async_computation | async-start | bytes 1048576 | tf_op jit(solution)/shard_map/all_to_all | solution.py:18
  156.6 14.9 %all-to-all-start.1 = ((f32[8,1,4096]{2,1,0:T(1,128)}), f32[8,1,4096]{2,1,0:T(1,128)S(1)}, u32[]{:S(2)}, u32[]{:S(2)}) async-start(f32[8,1,4096]{2,1,0:T(1,128)} %reshape.187), calls=%async_computation.1 | async-start | bytes 262144 | tf_op jit(solution)/shard_map/all_to_all | solution.py:18
  173.1 3.5 %copy-start.1 = (f32[16,4,64,256]{3,2,1,0:T(8,128)S(1)}, f32[16,4,64,256]{3,2,1,0:T(8,128)}, u32[]{:S(2)}) copy-start(f32[16,4,64,256]{3,2,1,0:T(8,128)} %get-tuple-element.8) | copy-start | bytes 12582916
  210.5 36.5 %all-to-all-start.3 = ((bf16[16,256,128]{1,2,0:T(8,128)(2,1)}), bf16[16,256,128]{1,2,0:T(8,128)(2,1)}, u32[]{:S(2)}, u32[]{:S(2)}) async-start(bf16[16,256,128]{1,2,0:T(8,128)(2,1)} %bitcast.63), calls=%async_computation.3 | async-start | bytes 2097152 | tf_op jit(solution)/shard_map/all_to_all | solution.py:46
Sparse Core Ops, SparseCore 0:
  11.8 115.3 all-gather.1
where the time goes:
time: 257 us; the launch traced here: 256 us
  waiting for transfers between devices  119 us (46%)
  local copies, waits for them, and re-layouts  37.5 us (15%)
  starting transfers between devices  28.8 us (11%)
  matrix products  25 us (10%)
  blocking collectives  17.2 us (7%)
  other arithmetic  14.4 us (6%)
  between operations  13.7 us (5%)
    all_gather x1, waiting for transfers between devices, body(): gathered_rows = lax.all_gather(own_rows, 'seq', axis=0, tiled=True)  80 us
    all_to_all x1, waiting for transfers between devices, sent_and_summed(): lax.all_to_all(pieces, axis, split_axis=0, concat_axis=0, tiled=True)  28.1 us
    all_to_all x2, starting transfers between devices, from_everyone(): lax.all_to_all(jnp.broadcast_to(shard[None], (devices, *shard.shape)), ax...  20.4 us
    all_to_all x1, blocking collectives, sent_and_summed(): lax.all_to_all(pieces, axis, split_axis=0, concat_axis=0, tiled=True)  17.2 us
    unnamed x20, local copies, waits for them, and re-layouts  14.2 us
    dot_general x1, matrix products, body(): product = jnp.dot(flat_rows, kv_weight, preferred_element_type=jnp.float32)  13.6 us
    all_to_all x2, waiting for transfers between devices, from_everyone(): lax.all_to_all(jnp.broadcast_to(shard[None], (devices, *shard.shape)), ax...  11 us
    all_to_all x1, starting transfers between devices, sent_and_summed(): lax.all_to_all(pieces, axis, split_axis=0, concat_axis=0, tiled=True)  8.36 us
  transfers between devices with their start and end apart: 4, of which 4 were waited for; matrix products, arithmetic and copies ran while one was open for 7% of the time, Pallas kernels for 0%

commit v1 on v0

v1 whole, which is shorter than its diff:
```python
import functools

import jax
import jax.numpy as jnp
from jax import lax
from jax.experimental import pallas as pl
from jax.experimental.pallas import tpu as pltpu
from jax.sharding import PartitionSpec as P

HD = 64
EPSILON = 1e-06
DEAD = -1e30
LANES = 128
CORES = 2
CHUNKS = 4
F32 = jnp.float32
BF16 = jnp.bfloat16


def normalise(src, gain, dst_at, total_rows):
    step = 16

    def one(i, carry):
        at = pl.ds(pl.multiple_of(i * step, step), step)
        rows = src[at, :].astype(F32)
        mean_square = jnp.mean(rows * rows, axis=-1, keepdims=True)
        dst_at[at, :] = (rows * lax.rsqrt(mean_square + EPSILON) * gain[...]).astype(BF16)
        return carry

    lax.fori_loop(0, total_rows // step, one, 0)


def kernel(
    table, states_hbm, enc_gain, dec_hbm, dec_gain, wq_hbm, wkv_hbm, wo_hbm, out_ref,
    raw, dec_raw, dec_rows, rows, wq, wkv, wo, kv, qbuf, num, peak, total,
    osend, orecv, lsend, lrecv, lpack, att, psend, precv, xsend, xrecv, first, second, hits,
    load_sem, rs, rr, ls, lr, ds, dr, qs, qr, os_, or_, ss, sr, ps, pr, xs, xr,
):
    shards, groups = lax.axis_size("seq"), lax.axis_size("qset")
    chips = shards // CORES
    me, g = lax.axis_index("seq"), lax.axis_index("qset")
    x, c = lax.div(me, CORES), lax.rem(me, CORES)
    plen, width = raw.shape
    questions, tokens, cols = qbuf.shape
    mine = questions // groups
    piece = plen // CHUNKS
    messages = (chips - 1) * CHUNKS // 2

    def seq_at(chip, core):
        return lax.rem(chip + 2 * chips, chips) * CORES + core

    right, left = seq_at(x + 1, c), seq_at(x - 1, c)
    other = 1 - c
    partner = seq_at(x, other)

    def load(i, src, dst):
        return pltpu.make_async_copy(src, dst, load_sem.at[i])

    loads = [
        load(0, states_hbm, raw),
        load(1, dec_hbm, dec_raw),
        load(2, wq_hbm, wq),
        load(3, wkv_hbm, wkv),
    ]
    for one in loads:
        one.start()
    wide = wo.shape[2]

    def wo_load(i):
        return load(4 + i, wo_hbm.at[:, pl.ds(pl.multiple_of(i * wide, wide), wide)], wo.at[i])

    lax.fori_loop(0, shards, lambda i, n: (wo_load(i).start(), n)[1], 0)

    barrier = pltpu.get_barrier_semaphore()

    def greet_seq(i, n):
        pl.semaphore_signal(barrier, inc=1, device_id={"seq": seq_at(x + i, c)})
        return n

    def greet_qset(i, n):
        pl.semaphore_signal(barrier, inc=1, device_id={"qset": lax.rem(g + i, groups)})
        return n

    pl.semaphore_signal(barrier, inc=1, device_id={"seq": partner})
    lax.fori_loop(1, chips, greet_seq, 0)
    lax.fori_loop(1, groups, greet_qset, 0)

    loads[0].wait()
    normalise(raw, enc_gain, rows.at[me], plen)
    pl.semaphore_wait(barrier, 1 + (chips - 1) + (groups - 1))

    def part(slot, chunk):
        return rows.at[slot, pl.ds(pl.multiple_of(chunk * piece, piece), piece), :]

    def right_copy(m, behind):
        at = part(seq_at(x - lax.div(m, CHUNKS) - behind, c), lax.rem(m, CHUNKS))
        return pltpu.make_async_remote_copy(at, at, rs.at[m], rr.at[m], device_id={"seq": right})

    def left_copy(m, behind):
        at = part(seq_at(x + lax.div(m, CHUNKS) + behind, c), CHUNKS - 1 - lax.rem(m, CHUNKS))
        return pltpu.make_async_remote_copy(at, at, ls.at[m], lr.at[m], device_id={"seq": left})

    def die_copy(k, slot, chunk):
        at = part(slot, chunk)
        return pltpu.make_async_remote_copy(at, at, ds.at[k], dr.at[k], device_id={"seq": partner})

    def from_left(m, core):
        return seq_at(x - lax.div(m, CHUNKS) - 1, core), lax.rem(m, CHUNKS)

    def from_right(m, core):
        return seq_at(x + lax.div(m, CHUNKS) + 1, core), CHUNKS - 1 - lax.rem(m, CHUNKS)

    def start_own(m, n):
        right_copy(m, 0).start()
        left_copy(m, 0).start()
        die_copy(m, me, m).start()
        return n

    lax.fori_loop(0, CHUNKS, start_own, 0)

    loads[1].wait()
    normalise(dec_raw, dec_gain, dec_rows, dec_raw.shape[0])
    loads[2].wait()
    queries = jnp.dot(dec_rows[...], wq[...], preferred_element_type=F32).astype(BF16)
    own_q = qbuf.at[pl.ds(g * mine, mine)]
    own_q[...] = queries.reshape(mine, tokens, cols)

    def query_copy(i):
        to = lax.rem(g + i, groups)
        return pltpu.make_async_remote_copy(
            own_q, own_q, qs.at[i], qr.at[i], device_id={"qset": to}
        )

    def query_arrival(i):
        at = qbuf.at[pl.ds(lax.rem(g - i + groups, groups) * mine, mine)]
        return pltpu.make_async_remote_copy(at, at, qs.at[i], qr.at[i], device_id={"qset": g})

    lax.fori_loop(1, groups, lambda i, n: (query_copy(i).start(), n)[1], 0)

    passages = table.shape[1]

    def find(q, n):
        def look(p, found):
            at0, at1, count = found
            hit = table[g, p] == q
            at0 = jnp.where(hit & (count == 0), p, at0)
            at1 = jnp.where(hit & (count == 1), p, at1)
            return at0, at1, count + hit.astype(jnp.int32)

        zero = jnp.int32(0)
        at0, at1, count = lax.fori_loop(0, passages, look, (zero, zero, zero))
        first[q], second[q], hits[q] = at0, at1, count
        return n

    lax.fori_loop(0, questions, find, 0)

    lane = lax.broadcasted_iota(jnp.int32, (1, LANES), 1)
    low = lane < HD

    def key_values(slots):
        together = jnp.concatenate([part(*s)[...] for s in slots], axis=0)
        result = jnp.dot(together, wkv[...], preferred_element_type=F32).astype(BF16)
        for i, (slot, chunk) in enumerate(slots):
            at = pl.ds(pl.multiple_of(chunk * piece, piece), piece)
            kv[slot, at, :] = result[i * piece : (i + 1) * piece]

    def attend(slot):
        asked = qbuf[table[g, slot]]
        for j in range(cols // LANES):
            at = slice(j * LANES, (j + 1) * LANES)
            pair = asked[:, at]
            none = jnp.zeros_like(pair)
            stacked = jnp.concatenate([jnp.where(low, pair, none), jnp.where(low, none, pair)], axis=0)
            keys = kv[slot, :, at]
            values = kv[slot, :, cols + j * LANES : cols + (j + 1) * LANES]
            scores = lax.dot_general(
                stacked, keys, (((1,), (1,)), ((), ())), preferred_element_type=F32
            )
            top = jnp.max(scores, axis=-1, keepdims=True)
            weights = jnp.exp(scores - top)
            summed = jnp.sum(weights, axis=-1, keepdims=True)
            product = jnp.dot(weights.astype(BF16), values, preferred_element_type=F32)
            num[slot, :, at] = jnp.where(low, product[:tokens], product[tokens:])
            peak[slot, :, at] = jnp.where(low, top[:tokens], top[tokens:])
            total[slot, :, at] = jnp.where(low, summed[:tokens], summed[tokens:])

    loads[3].wait()

    def own_values(m, n):
        key_values([(me, m)])
        die_copy(m, partner, m).wait_recv()
        key_values([(partner, m)])
        return n

    lax.fori_loop(0, CHUNKS, own_values, 0)

    def partner_part(m):
        die_copy(CHUNKS + m, *from_left(m, other)).wait_recv()
        die_copy(CHUNKS + messages + m, *from_right(m, other)).wait_recv()
        key_values([from_left(m, other), from_right(m, other)])

    def step(m, n):
        right_copy(m, 1).wait_recv()

        @pl.when(m + CHUNKS < messages)
        def _():
            right_copy(m + CHUNKS, 0).start()

        die_copy(CHUNKS + m, *from_left(m, c)).start()
        left_copy(m, 1).wait_recv()

        @pl.when(m + CHUNKS < messages)
        def _():
            left_copy(m + CHUNKS, 0).start()

        die_copy(CHUNKS + messages + m, *from_right(m, c)).start()
        key_values([from_left(m, c), from_right(m, c)])

        @pl.when(m > 0)
        def _():
            partner_part(m - 1)

        @pl.when(m == CHUNKS // 2)
        def _():
            lax.fori_loop(1, groups, lambda i, k: (query_arrival(i).wait_recv(), k)[1], 0)
            lax.fori_loop(0, CORES, lambda i, k: (attend(seq_at(x, i)), k)[1], 0)

        @pl.when((m >= CHUNKS) & (lax.rem(m, CHUNKS) == 0))
        def _():
            far = lax.div(m, CHUNKS)

            def both(i, k):
                attend(seq_at(x - far, i))
                attend(seq_at(x + far, i))
                return k

            lax.fori_loop(0, CORES, both, 0)

        return n

    lax.fori_loop(0, messages, step, 0)
    partner_part(messages - 1)
    lax.fori_loop(0, CORES, lambda i, k: (attend(seq_at(x + chips // 2, i)), k)[1], 0)

    lpack[...] = jnp.zeros_like(lpack)
    stride = LANES // 2 // groups
    pairs = cols // LANES

    def out_copy(i, own):
        to = lax.rem(g + i, groups)
        source = lax.rem(g - i + groups, groups)
        dst = orecv.at[source if own else g]
        return pltpu.make_async_remote_copy(
            osend.at[to], dst, os_.at[i], or_.at[i], device_id={"qset": to}
        )

    def lse_copy(i, own):
        to = lax.rem(g + i, groups)
        source = lax.rem(g - i + groups, groups)
        dst = lrecv.at[source if own else g]
        return pltpu.make_async_remote_copy(
            lsend.at[to], dst, ss.at[i], sr.at[i], device_id={"qset": to}
        )

    def merge(i, n):
        to = lax.rem(g + i, groups)
        for own in range(mine):
            q = to * mine + own
            at0, at1, count = first[q], second[q], hits[q]
            for j in range(pairs):
                at = slice(j * LANES, (j + 1) * LANES)
                top0 = jnp.where(count >= 1, peak[at0, :, at], DEAD)
                top1 = jnp.where(count >= 2, peak[at1, :, at], DEAD)
                top = jnp.maximum(top0, top1)
                scale0 = jnp.where(count >= 1, jnp.exp(top0 - top), 0.0)
                scale1 = jnp.where(count >= 2, jnp.exp(top1 - top), 0.0)
                mass = scale0 * total[at0, :, at] + scale1 * total[at1, :, at]
                mass = jnp.where(count >= 1, mass, 1.0)
                mix = (scale0 * num[at0, :, at] + scale1 * num[at1, :, at]) / mass
                osend[to, own * tokens : (own + 1) * tokens, at] = mix.astype(BF16)
                lse = jnp.where(count >= 1, top + jnp.log(mass), DEAD)
                spot = to * stride + own * pairs + j
                hit = (lane == spot) | (lane == HD + spot + stride // 2)
                lpack[:tokens, :] = jnp.where(hit, lse, lpack[:tokens, :])
        return n

    def merge_and_send(i, n):
        merge(i, n)
        out_copy(i, False).start()
        return n

    lax.fori_loop(1, groups, merge_and_send, 0)
    merge(0, 0)
    turned = jnp.transpose(lpack[...])
    lsend[...] = (turned[: LANES // 2] + turned[LANES // 2 :]).reshape(groups, stride, LANES)
    lax.fori_loop(1, groups, lambda i, n: (lse_copy(i, False).start(), n)[1], 0)
    lrecv[g] = lsend[g]
    orecv[g] = osend[g]

    for i in range(shards):
        wo_load(i).wait()

    def arrived(i, n):
        lse_copy(i, True).wait_recv()
        out_copy(i, True).wait_recv()
        return n

    lax.fori_loop(1, groups, arrived, 0)
    every = lrecv[...]
    top = jnp.max(every, axis=0, keepdims=True)
    share = jnp.exp(every - top)
    share = share / jnp.sum(share, axis=0, keepdims=True)
    share = share.reshape(groups * stride, LANES)
    lpack[...] = jnp.transpose(jnp.concatenate([share, share], axis=0))
    for own in range(mine):
        for j in range(pairs):
            at = slice(j * LANES, (j + 1) * LANES)
            here = slice(own * tokens, (own + 1) * tokens)
            mixed = jnp.zeros((tokens, LANES), F32)
            for source in range(groups):
                spot = source * stride + own * pairs + j
                odd = spot + stride // 2
                scale = jnp.where(
                    low, lpack[:tokens, spot : spot + 1], lpack[:tokens, odd : odd + 1]
                )
                mixed = mixed + scale * orecv[source, here, at].astype(F32)
            att[here, at] = mixed.astype(BF16)

    def product(chip, core):
        return jnp.dot(att[...], wo[chip * CORES + core], preferred_element_type=F32)

    def pair_copy(i):
        return pltpu.make_async_remote_copy(
            psend.at[i], precv.at[i], ps.at[i], pr.at[i], device_id={"seq": partner}
        )

    def sum_copy(i, own):
        to = lax.rem(x + i, chips)
        source = lax.rem(x - i + chips, chips)
        return pltpu.make_async_remote_copy(
            xsend.at[i], xrecv.at[i], xs.at[i], xr.at[i], device_id={"seq": seq_at(to, c)}
        )

    def to_partner(k, n):
        i = lax.rem(k + chips // 2, chips)
        psend[i] = product(lax.rem(x + i, chips), other).astype(BF16)
        pair_copy(i).start()
        return n

    lax.fori_loop(0, chips, to_partner, 0)

    def to_chip(k, n):
        i = lax.rem(k + chips // 2, chips)
        half = product(lax.rem(x + i, chips), c)
        pair_copy(i).wait_recv()
        xsend[i] = (half + precv[i].astype(F32)).astype(BF16)

        @pl.when(i > 0)
        def _():
            sum_copy(i, False).start()

        return n

    lax.fori_loop(0, chips, to_chip, 0)
    feature = pl.ds(pl.multiple_of(me * cols, cols), cols)
    result = dec_raw[:, feature].astype(F32) + xsend[0].astype(F32)
    for i in range(1, chips):
        sum_copy(i, True).wait_recv()
        result = result + xrecv[i].astype(F32)
    out_ref[...] = result.astype(BF16).reshape(out_ref.shape)

    def sent(m, n):
        right_copy(m, 0).wait_send()
        left_copy(m, 0).wait_send()
        return n

    lax.fori_loop(0, messages, sent, 0)
    lax.fori_loop(
        0, CHUNKS * chips, lambda k, n: (die_copy(k, me, 0).wait_send(), n)[1], 0
    )

    def sent_qset(i, n):
        query_copy(i).wait_send()
        out_copy(i, False).wait_send()
        lse_copy(i, False).wait_send()
        return n

    lax.fori_loop(1, groups, sent_qset, 0)
    lax.fori_loop(0, chips, lambda i, n: (pair_copy(i).wait_send(), n)[1], 0)
    lax.fori_loop(1, chips, lambda i, n: (sum_copy(i, False).wait_send(), n)[1], 0)


def body(
    states, enc_gain, dec_states, dec_gain, query_weight, key_value_weight, out_weight, question_of
):
    shards, groups = lax.axis_size("seq"), lax.axis_size("qset")
    chips = shards // CORES
    plen, width = states.shape[2:]
    mine, tokens = dec_states.shape[:2]
    cols = query_weight.shape[1]
    questions = mine * groups
    messages = (chips - 1) * CHUNKS // 2
    hbm = pl.BlockSpec(memory_space=pl.ANY)
    vmem = pl.BlockSpec(memory_space=pltpu.VMEM)
    smem = pl.BlockSpec(memory_space=pltpu.SMEM)
    dma = lambda n: pltpu.SemaphoreType.DMA((n,))
    return pl.pallas_call(
        kernel,
        out_shape=jax.ShapeDtypeStruct((mine, tokens, cols), BF16),
        in_specs=[smem, hbm, vmem, hbm, vmem, hbm, hbm, hbm],
        out_specs=vmem,
        scratch_shapes=[
            pltpu.VMEM((plen, width), BF16),
            pltpu.VMEM((mine * tokens, width), BF16),
            pltpu.VMEM((mine * tokens, width), BF16),
            pltpu.VMEM((shards, plen, width), BF16),
            pltpu.VMEM((width, cols), BF16),
            pltpu.VMEM((width, 2 * cols), BF16),
            pltpu.VMEM((shards, cols, cols), BF16),
            pltpu.VMEM((shards, plen, 2 * cols), BF16),
            pltpu.VMEM((questions, tokens, cols), BF16),
            pltpu.VMEM((shards, tokens, cols), F32),
            pltpu.VMEM((shards, tokens, cols), F32),
            pltpu.VMEM((shards, tokens, cols), F32),
            pltpu.VMEM((groups, mine * tokens, cols), BF16),
            pltpu.VMEM((groups, mine * tokens, cols), BF16),
            pltpu.VMEM((groups, LANES // 2 // groups, LANES), F32),
            pltpu.VMEM((groups, LANES // 2 // groups, LANES), F32),
            pltpu.VMEM((LANES, LANES), F32),
            pltpu.VMEM((mine * tokens, cols), BF16),
            pltpu.VMEM((chips, mine * tokens, cols), BF16),
            pltpu.VMEM((chips, mine * tokens, cols), BF16),
            pltpu.VMEM((chips, mine * tokens, cols), BF16),
            pltpu.VMEM((chips, mine * tokens, cols), BF16),
            pltpu.SMEM((questions,), jnp.int32),
            pltpu.SMEM((questions,), jnp.int32),
            pltpu.SMEM((questions,), jnp.int32),
            dma(4 + shards),
            dma(messages), dma(messages), dma(messages), dma(messages),
            dma(CHUNKS * chips), dma(CHUNKS * chips),
            dma(groups), dma(groups), dma(groups), dma(groups), dma(groups), dma(groups),
            dma(chips), dma(chips), dma(chips), dma(chips),
        ],
        compiler_params=pltpu.CompilerParams(
            collective_id=0, has_side_effects=True, vmem_limit_bytes=60 * 1024 * 1024
        ),
        name="reader_step",
    )(
        question_of[:, :, 0],
        states.reshape(plen, width),
        enc_gain.astype(F32).reshape(1, width),
        dec_states.reshape(mine * tokens, width),
        dec_gain.astype(F32).reshape(1, width),
        query_weight,
        key_value_weight.reshape(width, 2 * cols),
        out_weight,
    )


def solution(mesh):
    return jax.shard_map(
        body,
        mesh=mesh,
        in_specs=(
            P(("groups", "qset"), "seq", None, None),
            P(),
            P(("groups", "qset"), None, None),
            P(),
            P(None, "seq"),
            P(None, None, "seq"),
            P("seq", None),
            P("groups", None, None),
        ),
        out_specs=P(("groups", "qset"), None, "seq"),
        check_vma=False,
    )
```

time: 257 us -> 146 us (0.57)
  Pallas kernels: 0 us -> 136 us
  waiting for transfers between devices: 119 us -> 0 us
  local copies, waits for them, and re-layouts: 37.5 us -> 6.32 us
  starting transfers between devices: 28.8 us -> 0 us
  matrix products: 25 us -> 0 us
  blocking collectives: 17.2 us -> 0 us
  between operations: 13.7 us -> 0.01 us
  other arithmetic: 14.4 us -> 2.6 us
    pallas_call x0 -> x1, Pallas kernels: none -> 136 us  [body(): pl.pallas_call(kernel, out_shape=jax.ShapeDtypeStruct((mine, tokens, cols...]
    all_gather x1 -> x0, waiting for transfers between devices: 80 us -> none  [body(): gathered_rows = lax.all_gather(own_rows, 'seq', axis=0, tiled=True)]
    all_to_all x3 -> x0, waiting for transfers between devices: 39.1 us -> none  [the longest x1 28.1 us: sent_and_summed(): lax.all_to_all(pieces, axis, split_axis=0, concat_axis=0, tiled=True)]
    all_to_all x3 -> x0, starting transfers between devices: 28.8 us -> none  [the longest x2 20.4 us: from_everyone(): lax.all_to_all(jnp.broadcast_to(shard[None], (devices, *shard.shape)), ax...]
    dot_general x6 -> x0, matrix products: 25 us -> none  [the longest x1 13.6 us: body(): product = jnp.dot(flat_rows, kv_weight, preferred_element_type=jnp.float32)]
    all_to_all x1 -> x0, blocking collectives: 17.2 us -> none  [sent_and_summed(): lax.all_to_all(pieces, axis, split_axis=0, concat_axis=0, tiled=True)]
    slice x3 -> x0, local copies, waits for them, and re-layouts: 10.4 us -> none  [the longest x2 6.43 us: body(): local_keys[:, :, head_cols:].reshape(all_questions, -1, heads_here, HD)]
    unnamed x20 -> x2, local copies, waits for them, and re-layouts: 14.2 us -> 6.32 us
  transfers between devices with their start and end apart: 4 -> 0, of which waited for: 4 -> 0; matrix products, arithmetic and copies ran while one was open for 7% -> 0% of each run, Pallas kernels for 0% -> 0%
where the time goes in v1:
time: 146 us; the launch traced here: 145 us
  Pallas kernels  136 us (93%)
  local copies, waits for them, and re-layouts  6.32 us (4%)
  other arithmetic  2.6 us (2%)
    pallas_call x1, Pallas kernels, body(): pl.pallas_call(kernel, out_shape=jax.ShapeDtypeStruct((mine, tokens, cols...  136 us
    unnamed x2, local copies, waits for them, and re-layouts  6.32 us

profile of v1, /device:TPU:513, one launch (start us, length us, event | category | flops | bytes accessed | tf_op | source)
XLA Modules:
  0.0 145.4 jit_solution(1592129391733229089)
XLA Ops:
  0.0 1.3 reshape.26
  1.3 1.3 reshape.28
  2.6 4.8 %copy.9 = bf16[512,8,2,256]{3,1,2,0:T(8,128)(2,1)} copy(bf16[512,8,2,256]{3,2,1,0:T(2,128)(2,1)} %bitcast.8) | data formatting | bytes 8388608
  7.4 136.5 %reader_step.1 = bf16[2,64,256]{2,1,0:T(8,128)(2,1)} custom-call(s32[8,16]{1,0:T(8,128)} %bitcast.13, bf16[128,4096]{1,0:T(8,128)(2,1)} %bitcast.9, f32[1,4096]{1,0:T(1,128)} %bitcast.11, bf16[128,4096]{1,0:T(8,128)(2,1)} %bitcast.10, f32[1,4096]{1,0:T(1,128)} %bitcast.12, bf16[4096,256]{1,0:T(8,128)(2,1)} %wq_hbm.1, bf16[4096,512]{1,0:T(8,128)(2,1)} %bitcast.7, ...), custom_call_target="tpu_custom_call" | custom-call | tf_op jit(solution)/shard_map/reader_step/pallas_call | solution.py:407
  143.9 1.5 %copy.11 = bf16[2,64,256]{2,1,0:T(8,128)(2,1)} copy(bf16[2,64,256]{2,1,0:T(8,128)(2,1)} %reader_step.1) | data formatting | bytes 131072

commit v2 on v1

v2 whole, which is shorter than its diff:
```python
import functools

import jax
import jax.numpy as jnp
from jax import lax
from jax.experimental import pallas as pl
from jax.experimental.pallas import tpu as pltpu
from jax.sharding import PartitionSpec as P

HD = 64
EPSILON = 1e-06
DEAD = -1e30
LANES = 128
CORES = 2
CHUNKS = 4
F32 = jnp.float32
BF16 = jnp.bfloat16


def normalise(src, gain, dst_at, total_rows):
    step = 16

    def one(i, carry):
        at = pl.ds(pl.multiple_of(i * step, step), step)
        rows = src[at, :].astype(F32)
        mean_square = jnp.mean(rows * rows, axis=-1, keepdims=True)
        dst_at[at, :] = (rows * lax.rsqrt(mean_square + EPSILON) * gain[...]).astype(BF16)
        return carry

    lax.fori_loop(0, total_rows // step, one, 0)


def kernel(
    table, states_hbm, enc_gain, dec_hbm, dec_gain, wq_hbm, wkv_hbm, wo_hbm, out_ref,
    raw, dec_raw, dec_rows, rows, wq, wkv_in, wkv, wo, kv, qbuf, num, peak, total,
    osend, orecv, lsend, lrecv, shares, att, half, psend, precv, xsend, xrecv, gains,
    first, second, hits,
    load_sem, rs, rr, ls, lr, ds, dr, qs, qr, os_, or_, ss, sr, ps, pr, xs, xr, rising, falling,
):
    shards, groups = lax.axis_size("seq"), lax.axis_size("qset")
    chips = shards // CORES
    me, g = lax.axis_index("seq"), lax.axis_index("qset")
    x, c = lax.div(me, CORES), lax.rem(me, CORES)
    plen, width = raw.shape
    questions, tokens, cols = qbuf.shape
    mine = questions // groups
    piece = plen // CHUNKS
    messages = (chips - 1) * CHUNKS // 2

    def seq_at(chip, core):
        return lax.rem(chip + 2 * chips, chips) * CORES + core

    right, left = seq_at(x + 1, c), seq_at(x - 1, c)
    other = 1 - c
    partner = seq_at(x, other)

    def load(i, src, dst):
        return pltpu.make_async_copy(src, dst, load_sem.at[i])

    states_load = load(0, states_hbm, raw)
    dec_load = load(1, dec_hbm, dec_raw)
    wq_load = load(2, wq_hbm, wq)
    wkv_load = load(3, wkv_hbm, wkv_in)

    def wo_load(i):
        chip, core = lax.div(i, CORES), lax.rem(i, CORES)
        src = wo_hbm.at[:, pl.ds(pl.multiple_of(i * cols, cols), cols)]
        dst = wo.at[core, :, pl.ds(pl.multiple_of(chip * cols, cols), cols)]
        return load(4 + i, src, dst)

    states_load.start()

    barrier = pltpu.get_barrier_semaphore()
    above, below = g + 1, g - 1

    def greet_seq(i, n):
        pl.semaphore_signal(barrier, inc=1, device_id={"seq": seq_at(x + i, c)})
        return n

    pl.semaphore_signal(barrier, inc=1, device_id={"seq": partner})
    lax.fori_loop(1, chips, greet_seq, 0)

    def if_above(do):
        pl.when(g < groups - 1)(do)

    def if_below(do):
        pl.when(g > 0)(do)

    if_above(lambda: pl.semaphore_signal(barrier, inc=1, device_id={"qset": above}))
    if_below(lambda: pl.semaphore_signal(barrier, inc=1, device_id={"qset": below}))

    gains[0:1, :] = enc_gain[...].astype(F32).reshape(1, width)
    gains[8:9, :] = dec_gain[...].astype(F32).reshape(1, width)
    states_load.wait()
    dec_load.start()
    wq_load.start()
    wkv_load.start()
    lax.fori_loop(0, shards, lambda i, n: (wo_load(i).start(), n)[1], 0)
    normalise(raw, gains.at[0:1, :], rows.at[me], plen)
    rows_beside = lax.div(g + groups - 1, groups) + 1 - lax.div(g + 1, groups)
    pl.semaphore_wait(barrier, chips + rows_beside)

    def part(slot, chunk):
        return rows.at[slot, pl.ds(pl.multiple_of(chunk * piece, piece), piece), :]

    def right_copy(m, behind):
        at = part(seq_at(x - lax.div(m, CHUNKS) - behind, c), lax.rem(m, CHUNKS))
        return pltpu.make_async_remote_copy(at, at, rs.at[m], rr.at[m], device_id={"seq": right})

    def left_copy(m, behind):
        at = part(seq_at(x + lax.div(m, CHUNKS) + behind, c), CHUNKS - 1 - lax.rem(m, CHUNKS))
        return pltpu.make_async_remote_copy(at, at, ls.at[m], lr.at[m], device_id={"seq": left})

    def die_copy(k, slot, chunk):
        at = part(slot, chunk)
        return pltpu.make_async_remote_copy(at, at, ds.at[k], dr.at[k], device_id={"seq": partner})

    def from_left(m, core):
        return seq_at(x - lax.div(m, CHUNKS) - 1, core), lax.rem(m, CHUNKS)

    def from_right(m, core):
        return seq_at(x + lax.div(m, CHUNKS) + 1, core), CHUNKS - 1 - lax.rem(m, CHUNKS)

    def start_own(m, n):
        right_copy(m, 0).start()
        left_copy(m, 0).start()
        die_copy(m, me, m).start()
        return n

    lax.fori_loop(0, CHUNKS, start_own, 0)

    dec_load.wait()
    normalise(dec_raw, gains.at[8:9, :], dec_rows, dec_raw.shape[0])
    wq_load.wait()
    queries = jnp.dot(dec_rows[...], wq[...], preferred_element_type=F32).astype(BF16)
    own_q = qbuf.at[pl.ds(g * mine, mine)]
    own_q[...] = queries.reshape(mine, tokens, cols)

    def query_copy(i):
        to = lax.rem(g + i, groups)
        return pltpu.make_async_remote_copy(
            own_q, own_q, qs.at[i], qr.at[i], device_id={"qset": to}
        )

    def query_arrival(i):
        at = qbuf.at[pl.ds(lax.rem(g - i + groups, groups) * mine, mine)]
        return pltpu.make_async_remote_copy(at, at, qs.at[i], qr.at[i], device_id={"qset": g})

    passages = table.shape[1]

    def find(q, n):
        def look(p, found):
            at0, at1, count = found
            hit = table[g, p] == q
            at0 = jnp.where(hit & (count == 0), p, at0)
            at1 = jnp.where(hit & (count == 1), p, at1)
            return at0, at1, count + hit.astype(jnp.int32)

        zero = jnp.int32(0)
        at0, at1, count = lax.fori_loop(0, passages, look, (zero, zero, zero))
        first[q], second[q], hits[q] = at0, at1, count
        return n

    lax.fori_loop(0, questions, find, 0)

    lane = lax.broadcasted_iota(jnp.int32, (1, LANES), 1)
    low = lane < HD

    def key_values(slots):
        together = jnp.concatenate([part(*s)[...] for s in slots], axis=0)
        result = jnp.dot(together, wkv[...], preferred_element_type=F32).astype(BF16)
        for i, (slot, chunk) in enumerate(slots):
            at = pl.ds(pl.multiple_of(chunk * piece, piece), piece)
            kv[slot, at, :] = result[i * piece : (i + 1) * piece]

    def attend(slot):
        asked = qbuf[table[g, slot]]
        for j in range(cols // LANES):
            at = slice(j * LANES, (j + 1) * LANES)
            pair = asked[:, at]
            none = jnp.zeros_like(pair)
            stacked = jnp.concatenate([jnp.where(low, pair, none), jnp.where(low, none, pair)], axis=0)
            keys = kv[slot, :, at]
            values = kv[slot, :, cols + j * LANES : cols + (j + 1) * LANES]
            scores = lax.dot_general(
                stacked, keys, (((1,), (1,)), ((), ())), preferred_element_type=F32
            )
            top = jnp.max(scores, axis=-1, keepdims=True)
            weights = jnp.exp(scores - top)
            summed = jnp.sum(weights, axis=-1, keepdims=True)
            product = jnp.dot(weights.astype(BF16), values, preferred_element_type=F32)
            num[slot, :, at] = jnp.where(low, product[:tokens], product[tokens:])
            peak[slot, :, at] = jnp.where(low, top[:tokens], top[tokens:])
            total[slot, :, at] = jnp.where(low, summed[:tokens], summed[tokens:])

    wkv_load.wait()
    block = 64

    def unzip(i, n):
        at = pl.ds(pl.multiple_of(i * block, block), block)
        wkv[at, :cols] = wkv_in[at, 0, :]
        wkv[at, cols:] = wkv_in[at, 1, :]
        return n

    lax.fori_loop(0, width // block, unzip, 0)

    def own_values(m, n):
        key_values([(me, m)])
        die_copy(m, partner, m).wait_recv()
        key_values([(partner, m)])
        return n

    lax.fori_loop(0, CHUNKS, own_values, 0)

    def partner_part(m):
        die_copy(CHUNKS + m, *from_left(m, other)).wait_recv()
        die_copy(CHUNKS + messages + m, *from_right(m, other)).wait_recv()
        key_values([from_left(m, other), from_right(m, other)])

    def step(m, n):
        right_copy(m, 1).wait_recv()

        @pl.when(m + CHUNKS < messages)
        def _():
            right_copy(m + CHUNKS, 0).start()

        die_copy(CHUNKS + m, *from_left(m, c)).start()
        left_copy(m, 1).wait_recv()

        @pl.when(m + CHUNKS < messages)
        def _():
            left_copy(m + CHUNKS, 0).start()

        die_copy(CHUNKS + messages + m, *from_right(m, c)).start()
        key_values([from_left(m, c), from_right(m, c)])

        @pl.when(m > 0)
        def _():
            partner_part(m - 1)

        @pl.when(m == CHUNKS // 2)
        def _():
            if_above(lambda: pl.semaphore_wait(falling, 1))
            if_below(lambda: pl.semaphore_signal(falling, inc=1, device_id={"qset": below}))
            lax.fori_loop(1, groups, lambda i, k: (query_copy(i).start(), k)[1], 0)

        @pl.when(m == messages // 2)
        def _():
            lax.fori_loop(1, groups, lambda i, k: (query_arrival(i).wait_recv(), k)[1], 0)
            lax.fori_loop(0, CORES, lambda i, k: (attend(seq_at(x, i)), k)[1], 0)

        for far in range(1, chips // 2):

            @pl.when(m == max(far * CHUNKS, messages // 2 + far))
            def _():
                def both(i, k):
                    attend(seq_at(x - far, i))
                    attend(seq_at(x + far, i))
                    return k

                lax.fori_loop(0, CORES, both, 0)

        return n

    if_below(lambda: pl.semaphore_wait(rising, 1))
    if_above(lambda: pl.semaphore_signal(rising, inc=1, device_id={"qset": above}))
    lax.fori_loop(0, messages, step, 0)
    attend(seq_at(x + chips // 2, c))
    partner_part(messages - 1)
    attend(seq_at(x + chips // 2, other))

    pairs = cols // LANES
    odd_row = 4
    lse_rows = lsend.shape[2]

    def alternate(k, n):
        reach = lax.div(k + 1, 2)
        return n // 2 - reach + 2 * reach * lax.rem(k, 2)

    def out_copy(own, i, arrival):
        to = lax.rem(g + i, groups)
        source = lax.rem(g - i + groups, groups)
        at = own * groups + i
        return pltpu.make_async_remote_copy(
            osend.at[own, to],
            orecv.at[own, source if arrival else g],
            os_.at[at], or_.at[at], device_id={"qset": to},
        )

    def lse_copy(own, i, arrival):
        to = lax.rem(g + i, groups)
        source = lax.rem(g - i + groups, groups)
        at = own * groups + i
        return pltpu.make_async_remote_copy(
            lsend.at[own, to],
            lrecv.at[own, source if arrival else g],
            ss.at[at], sr.at[at], device_id={"qset": to},
        )

    def merge(own, to, mix_at, lse_at):
        q = to * mine + own
        at0, at1, count = first[q], second[q], hits[q]
        packed = jnp.zeros((tokens, LANES), F32)
        for j in range(pairs):
            at = slice(j * LANES, (j + 1) * LANES)
            top0 = jnp.where(count >= 1, peak[at0, :, at], DEAD)
            top1 = jnp.where(count >= 2, peak[at1, :, at], DEAD)
            top = jnp.maximum(top0, top1)
            scale0 = jnp.where(count >= 1, jnp.exp(top0 - top), 0.0)
            scale1 = jnp.where(count >= 2, jnp.exp(top1 - top), 0.0)
            mass = scale0 * total[at0, :, at] + scale1 * total[at1, :, at]
            mass = jnp.where(count >= 1, mass, 1.0)
            mix = (scale0 * num[at0, :, at] + scale1 * num[at1, :, at]) / mass
            mix_at[:, at] = mix.astype(BF16)
            lse = jnp.where(count >= 1, top + jnp.log(mass), DEAD)
            packed = jnp.where((lane == j) | (lane == HD + odd_row + j), lse, packed)
        turned = jnp.transpose(packed)
        lse_at[:, :tokens] = turned[:lse_rows] + turned[HD : HD + lse_rows]

    lsend[...] = jnp.zeros_like(lsend)
    lrecv_pad = jnp.zeros(lrecv.shape[2:], F32)

    def merge_and_send(own):
        def one(k, n):
            i = alternate(k, groups)
            to = lax.rem(g + i, groups)
            merge(own, to, osend.at[own, to], lsend.at[own, to])
            lse_copy(own, i, False).start()
            out_copy(own, i, False).start()
            return n

        lax.fori_loop(0, groups - 1, one, 0)

    for own in range(mine):
        merge_and_send(own)
    for own in range(mine):
        lrecv[own, g] = lrecv_pad
        merge(own, g, orecv.at[own, g], lrecv.at[own, g])
    lax.fori_loop(0, shards, lambda i, n: (wo_load(i).wait(), n)[1], 0)

    def pair_copy(own):
        return pltpu.make_async_remote_copy(
            psend.at[own], precv.at[own], ps.at[own], pr.at[own], device_id={"seq": partner}
        )

    def chip_part(chip):
        return pl.ds(pl.multiple_of(chip * cols, cols), cols)

    def sum_copy(own, i):
        to = lax.rem(x + i, chips)
        at = own * chips + i
        return pltpu.make_async_remote_copy(
            xsend.at[own, :, chip_part(to)], xrecv.at[own, i],
            xs.at[at], xr.at[at], device_id={"seq": seq_at(to, c)},
        )

    def project(own):
        def arrived(k, n):
            i = alternate(k, groups)
            lse_copy(own, i, True).wait_recv()
            out_copy(own, i, True).wait_recv()
            return n

        lax.fori_loop(0, groups - 1, arrived, 0)
        every = lrecv[own]
        top = jnp.max(every, axis=0, keepdims=True)
        share = jnp.exp(every - top)
        share = share / jnp.sum(share, axis=0, keepdims=True)
        shares[...] = jnp.transpose(share.reshape(groups * lse_rows, LANES))
        for j in range(pairs):
            at = slice(j * LANES, (j + 1) * LANES)
            mixed = jnp.zeros((tokens, LANES), F32)
            for source in range(groups):
                even, odd = source * lse_rows + j, source * lse_rows + odd_row + j
                scale = jnp.where(
                    low, shares[:tokens, even : even + 1], shares[:tokens, odd : odd + 1]
                )
                mixed = mixed + scale * orecv[own, source, :, at].astype(F32)
            att[:, at] = mixed.astype(BF16)

        psend[own] = jnp.dot(att[...], wo[other], preferred_element_type=F32).astype(BF16)
        pair_copy(own).start()
        half[...] = jnp.dot(att[...], wo[c], preferred_element_type=F32)
        pair_copy(own).wait_recv()

        def add(i):
            at = chip_part(lax.rem(x + i, chips))
            xsend[own, :, at] = (half[:, at] + precv[own, :, at].astype(F32)).astype(BF16)

        def to_chip(k, n):
            i = alternate(k, chips)
            add(i)
            sum_copy(own, i).start()
            return n

        lax.fori_loop(0, chips - 1, to_chip, 0)
        add(0)

    for own in range(mine):
        project(own)

    feature = pl.ds(pl.multiple_of(me * cols, cols), cols)
    for own in range(mine):
        here = slice(own * tokens, (own + 1) * tokens)
        result = dec_raw[here, feature].astype(F32) + xsend[own, :, chip_part(x)].astype(F32)
        for i in range(1, chips):
            sum_copy(own, i).wait_recv()
            result = result + xrecv[own, i].astype(F32)
        out_ref[own] = result.astype(BF16)

    def sent(m, n):
        right_copy(m, 0).wait_send()
        left_copy(m, 0).wait_send()
        return n

    lax.fori_loop(0, messages, sent, 0)
    lax.fori_loop(
        0, CHUNKS * chips, lambda k, n: (die_copy(k, me, 0).wait_send(), n)[1], 0
    )

    lax.fori_loop(1, groups, lambda i, n: (query_copy(i).wait_send(), n)[1], 0)
    for own in range(mine):

        def sent_qset(i, n):
            out_copy(own, i, False).wait_send()
            lse_copy(own, i, False).wait_send()
            return n

        lax.fori_loop(1, groups, sent_qset, 0)
        pair_copy(own).wait_send()
        lax.fori_loop(1, chips, lambda i, n: (sum_copy(own, i).wait_send(), n)[1], 0)


def body(
    states, enc_gain, dec_states, dec_gain, query_weight, key_value_weight, out_weight, question_of
):
    shards, groups = lax.axis_size("seq"), lax.axis_size("qset")
    chips = shards // CORES
    plen, width = states.shape[2:]
    mine, tokens = dec_states.shape[:2]
    cols = query_weight.shape[1]
    questions = mine * groups
    messages = (chips - 1) * CHUNKS // 2
    hbm = pl.BlockSpec(memory_space=pl.ANY)
    vmem = pl.BlockSpec(memory_space=pltpu.VMEM)
    smem = pl.BlockSpec(memory_space=pltpu.SMEM)
    dma = lambda n: pltpu.SemaphoreType.DMA((n,))
    return pl.pallas_call(
        kernel,
        out_shape=jax.ShapeDtypeStruct((mine, tokens, cols), BF16),
        in_specs=[smem, hbm, vmem, hbm, vmem, hbm, hbm, hbm],
        out_specs=vmem,
        scratch_shapes=[
            pltpu.VMEM((plen, width), BF16),
            pltpu.VMEM((mine * tokens, width), BF16),
            pltpu.VMEM((mine * tokens, width), BF16),
            pltpu.VMEM((shards, plen, width), BF16),
            pltpu.VMEM((width, cols), BF16),
            pltpu.VMEM((width, 2, cols), BF16),
            pltpu.VMEM((width, 2 * cols), BF16),
            pltpu.VMEM((CORES, cols, chips * cols), BF16),
            pltpu.VMEM((shards, plen, 2 * cols), BF16),
            pltpu.VMEM((questions, tokens, cols), BF16),
            pltpu.VMEM((shards, tokens, cols), F32),
            pltpu.VMEM((shards, tokens, cols), F32),
            pltpu.VMEM((shards, tokens, cols), F32),
            pltpu.VMEM((mine, groups, tokens, cols), BF16),
            pltpu.VMEM((mine, groups, tokens, cols), BF16),
            pltpu.VMEM((mine, groups, 8, LANES), F32),
            pltpu.VMEM((mine, groups, 8, LANES), F32),
            pltpu.VMEM((LANES, groups * 8), F32),
            pltpu.VMEM((tokens, cols), BF16),
            pltpu.VMEM((tokens, chips * cols), F32),
            pltpu.VMEM((mine, tokens, chips * cols), BF16),
            pltpu.VMEM((mine, tokens, chips * cols), BF16),
            pltpu.VMEM((mine, tokens, chips * cols), BF16),
            pltpu.VMEM((mine, chips, tokens, cols), BF16),
            pltpu.VMEM((16, width), F32),
            pltpu.SMEM((questions,), jnp.int32),
            pltpu.SMEM((questions,), jnp.int32),
            pltpu.SMEM((questions,), jnp.int32),
            dma(4 + shards),
            dma(messages), dma(messages), dma(messages), dma(messages),
            dma(CHUNKS * chips), dma(CHUNKS * chips),
            dma(groups), dma(groups),
            dma(mine * groups), dma(mine * groups), dma(mine * groups), dma(mine * groups),
            dma(mine), dma(mine), dma(mine * chips), dma(mine * chips),
            pltpu.SemaphoreType.REGULAR, pltpu.SemaphoreType.REGULAR,
        ],
        compiler_params=pltpu.CompilerParams(
            collective_id=0, has_side_effects=True, vmem_limit_bytes=60 * 1024 * 1024
        ),
        name="reader_step",
    )(
        question_of[:, :, 0],
        states.reshape(plen, width),
        enc_gain,
        dec_states.reshape(mine * tokens, width),
        dec_gain,
        query_weight,
        key_value_weight,
        out_weight,
    )


def solution(mesh):
    return jax.shard_map(
        body,
        mesh=mesh,
        in_specs=(
            P(("groups", "qset"), "seq", None, None),
            P(),
            P(("groups", "qset"), None, None),
            P(),
            P(None, "seq"),
            P(None, None, "seq"),
            P("seq", None),
            P("groups", None, None),
        ),
        out_specs=P(("groups", "qset"), None, "seq"),
        check_vma=False,
    )
```

time: 146 us -> 141 us (0.966)
  local copies, waits for them, and re-layouts: 6.32 us -> 1.47 us
  Pallas kernels: 136 us -> 139 us
  other arithmetic: 2.6 us -> 0 us
    unnamed x2 -> x1, local copies, waits for them, and re-layouts: 6.32 us -> 1.47 us
    reshape x2 -> x0, other arithmetic: 2.6 us -> none  [the longest x1 1.3 us: body(): enc_gain.astype(F32).reshape(1, width)]
    pallas_call x1, Pallas kernels: 136 us -> 139 us  [body(): pl.pallas_call(kernel, out_shape=jax.ShapeDtypeStruct((mine, tokens, cols...]
where the time goes in v2:
time: 141 us
  Pallas kernels  139 us (99%)
  local copies, waits for them, and re-layouts  1.47 us (1%)
    pallas_call x1, Pallas kernels, body(): pl.pallas_call(kernel, out_shape=jax.ShapeDtypeStruct((mine, tokens, cols...  139 us

profile of v2, /device:TPU:513, one launch (start us, length us, event | category | flops | bytes accessed | tf_op | source)
XLA Modules:
  0.0 140.5 jit_solution(3588068018162258244)
XLA Ops:
  0.0 139.1 %reader_step.1 = bf16[2,64,256]{2,1,0:T(8,128)(2,1)} custom-call(s32[8,16]{1,0:T(8,128)} %bitcast.5, bf16[128,4096]{1,0:T(8,128)(2,1)} %bitcast.3, bf16[4096]{0:T(1024)(128)(2,1)} %enc_gain.1, bf16[128,4096]{1,0:T(8,128)(2,1)} %bitcast.4, bf16[4096]{0:T(1024)(128)(2,1)} %dec_gain.1, bf16[4096,256]{1,0:T(8,128)(2,1)} %wq_hbm.1, ...), custom_call_target="tpu_custom_call" | custom-call | tf_op jit(solution)/shard_map/reader_step/pallas_call | solution.py:448
  139.1 1.5 %copy.10 = bf16[2,64,256]{2,1,0:T(8,128)(2,1)} copy(bf16[2,64,256]{2,1,0:T(8,128)(2,1)} %reader_step.1) | data formatting | bytes 131072

commit v3 on v2

--- a/solution.py
+++ b/solution.py
@@ -13,6 +13,8 @@
 LANES = 128
 CORES = 2
 CHUNKS = 4
+LAG = 4
+PARTS = 2
 F32 = jnp.float32
 BF16 = jnp.bfloat16
 
@@ -73,20 +75,19 @@
     barrier = pltpu.get_barrier_semaphore()
     above, below = g + 1, g - 1
 
-    def greet_seq(i, n):
-        pl.semaphore_signal(barrier, inc=1, device_id={"seq": seq_at(x + i, c)})
-        return n
-
-    pl.semaphore_signal(barrier, inc=1, device_id={"seq": partner})
-    lax.fori_loop(1, chips, greet_seq, 0)
-
     def if_above(do):
         pl.when(g < groups - 1)(do)
 
     def if_below(do):
         pl.when(g > 0)(do)
 
-    if_above(lambda: pl.semaphore_signal(barrier, inc=1, device_id={"qset": above}))
+    pl.semaphore_signal(barrier, inc=1, device_id={"seq": left})
+    pl.semaphore_signal(barrier, inc=1, device_id={"seq": right})
+
+    @pl.when(c == 1)
+    def _():
+        pl.semaphore_signal(barrier, inc=1, device_id={"seq": partner})
+
     if_below(lambda: pl.semaphore_signal(barrier, inc=1, device_id={"qset": below}))
 
     gains[0:1, :] = enc_gain[...].astype(F32).reshape(1, width)
@@ -97,8 +98,7 @@
     wkv_load.start()
     lax.fori_loop(0, shards, lambda i, n: (wo_load(i).start(), n)[1], 0)
     normalise(raw, gains.at[0:1, :], rows.at[me], plen)
-    rows_beside = lax.div(g + groups - 1, groups) + 1 - lax.div(g + 1, groups)
-    pl.semaphore_wait(barrier, chips + rows_beside)
+    pl.semaphore_wait(barrier, 2 + (1 - c) + 1 - lax.div(g + 1, groups))
 
     def part(slot, chunk):
         return rows.at[slot, pl.ds(pl.multiple_of(chunk * piece, piece), piece), :]
@@ -124,17 +124,27 @@
     def start_own(m, n):
         right_copy(m, 0).start()
         left_copy(m, 0).start()
-        die_copy(m, me, m).start()
+
+        @pl.when(c == 0)
+        def _():
+            die_copy(m, me, m).start()
+
         return n
 
     lax.fori_loop(0, CHUNKS, start_own, 0)
 
-    dec_load.wait()
-    normalise(dec_raw, gains.at[8:9, :], dec_rows, dec_raw.shape[0])
-    wq_load.wait()
-    queries = jnp.dot(dec_rows[...], wq[...], preferred_element_type=F32).astype(BF16)
+    @pl.when(g == 0)
+    def _():
+        pl.semaphore_signal(rising, inc=1, device_id={"qset": above})
+
     own_q = qbuf.at[pl.ds(g * mine, mine)]
-    own_q[...] = queries.reshape(mine, tokens, cols)
+
+    def own_queries():
+        dec_load.wait()
+        normalise(dec_raw, gains.at[8:9, :], dec_rows, dec_raw.shape[0])
+        wq_load.wait()
+        queries = jnp.dot(dec_rows[...], wq[...], preferred_element_type=F32).astype(BF16)
+        own_q[...] = queries.reshape(mine, tokens, cols)
 
     def query_copy(i):
         to = lax.rem(g + i, groups)
@@ -160,8 +170,6 @@
         at0, at1, count = lax.fori_loop(0, passages, look, (zero, zero, zero))
         first[q], second[q], hits[q] = at0, at1, count
         return n
-
-    lax.fori_loop(0, questions, find, 0)
 
     lane = lax.broadcasted_iota(jnp.int32, (1, LANES), 1)
     low = lane < HD
@@ -204,19 +212,28 @@
 
     lax.fori_loop(0, width // block, unzip, 0)
 
-    def own_values(m, n):
-        key_values([(me, m)])
-        die_copy(m, partner, m).wait_recv()
-        key_values([(partner, m)])
-        return n
-
-    lax.fori_loop(0, CHUNKS, own_values, 0)
+    def whole_values(slot):
+        result = jnp.dot(rows[slot], wkv[...], preferred_element_type=F32)
+        kv[slot] = result.astype(BF16)
 
     def partner_part(m):
         die_copy(CHUNKS + m, *from_left(m, other)).wait_recv()
         die_copy(CHUNKS + messages + m, *from_right(m, other)).wait_recv()
         key_values([from_left(m, other), from_right(m, other)])
 
+    def die_right(m):
+        die_copy(CHUNKS + m, *from_left(m, c)).start()
+
+    def die_left(m):
+        die_copy(CHUNKS + messages + m, *from_right(m, c)).start()
+
+    hold = 2
+    catch = messages - 4
+    partner_at = min(LAG, catch)
+
+    def part_done(m):
+        return m + LAG if m + LAG < catch else max(catch, m + 1)
+
     def step(m, n):
         right_copy(m, 1).wait_recv()
 
@@ -224,26 +241,88 @@
         def _():
             right_copy(m + CHUNKS, 0).start()
 
-        die_copy(CHUNKS + m, *from_left(m, c)).start()
+        @pl.when((1 - c) * messages + m > hold)
+        def _():
+            die_right(m)
+
         left_copy(m, 1).wait_recv()
 
         @pl.when(m + CHUNKS < messages)
         def _():
             left_copy(m + CHUNKS, 0).start()
 
-        die_copy(CHUNKS + messages + m, *from_right(m, c)).start()
+        @pl.when((1 - c) * messages + m > hold)
+        def _():
+            die_left(m)
+
+        @pl.when(m == 0)
+        def _():
+            whole_values(me)
+
         key_values([from_left(m, c), from_right(m, c)])
 
-        @pl.when(m > 0)
-        def _():
-            partner_part(m - 1)
-
-        @pl.when(m == CHUNKS // 2)
-        def _():
+        @pl.when(m == 1)
+        def _():
+            own_queries()
+            if_below(lambda: pl.semaphore_wait(rising, 1))
+
+            @pl.when(g > 0)
+            def _():
+                if_above(
+                    lambda: pl.semaphore_signal(rising, inc=1, device_id={"qset": above})
+                )
+
+        @pl.when(m == hold)
+        def _():
+            @pl.when(c == 1)
+            def _():
+                die_copy(0, partner, 0).wait_recv()
+                lax.fori_loop(0, CHUNKS, lambda k, t: (die_copy(k, me, k).start(), t)[1], 0)
+
+                def late(k, t):
+                    die_right(k)
+                    die_left(k)
+                    return t
+
+                lax.fori_loop(0, hold + 1, late, 0)
+
             if_above(lambda: pl.semaphore_wait(falling, 1))
             if_below(lambda: pl.semaphore_signal(falling, inc=1, device_id={"qset": below}))
             lax.fori_loop(1, groups, lambda i, k: (query_copy(i).start(), k)[1], 0)
 
+        @pl.when(m == hold + 1)
+        def _():
+            lax.fori_loop(0, questions, find, 0)
+
+        @pl.when(m == partner_at)
+        def _():
+            @pl.when(c == 0)
+            def _():
+                die_copy(0, partner, 0).wait_recv()
+
+            lax.fori_loop(
+                1, CHUNKS, lambda k, t: (die_copy(k, partner, k).wait_recv(), t)[1], 0
+            )
+            whole_values(partner)
+
+        if catch > LAG:
+
+            @pl.when(m >= LAG)
+            def _():
+                @pl.when(m < catch)
+                def _():
+                    partner_part(m - LAG)
+
+        @pl.when(m == catch)
+        def _():
+            lax.fori_loop(
+                max(0, catch - LAG), catch, lambda k, t: (partner_part(k), t)[1], 0
+            )
+
+        @pl.when(m > catch)
+        def _():
+            partner_part(m - 1)
+
         @pl.when(m == messages // 2)
         def _():
             lax.fori_loop(1, groups, lambda i, k: (query_arrival(i).wait_recv(), k)[1], 0)
@@ -251,7 +330,7 @@
 
         for far in range(1, chips // 2):
 
-            @pl.when(m == max(far * CHUNKS, messages // 2 + far))
+            @pl.when(m == max(part_done(far * CHUNKS - 1), messages // 2 + far))
             def _():
                 def both(i, k):
                     attend(seq_at(x - far, i))
@@ -262,11 +341,9 @@
 
         return n
 
-    if_below(lambda: pl.semaphore_wait(rising, 1))
-    if_above(lambda: pl.semaphore_signal(rising, inc=1, device_id={"qset": above}))
     lax.fori_loop(0, messages, step, 0)
+    partner_part(messages - 1)
     attend(seq_at(x + chips // 2, c))
-    partner_part(messages - 1)
     attend(seq_at(x + chips // 2, other))
 
     pairs = cols // LANES
@@ -277,13 +354,16 @@
         reach = lax.div(k + 1, 2)
         return n // 2 - reach + 2 * reach * lax.rem(k, 2)
 
-    def out_copy(own, i, arrival):
+    short = tokens // PARTS
+
+    def out_copy(own, cut, i, arrival):
         to = lax.rem(g + i, groups)
         source = lax.rem(g - i + groups, groups)
-        at = own * groups + i
+        at = (own * PARTS + cut) * groups + i
+        here = pl.ds(cut * short, short)
         return pltpu.make_async_remote_copy(
-            osend.at[own, to],
-            orecv.at[own, source if arrival else g],
+            osend.at[own, to, here],
+            orecv.at[own, source if arrival else g, here],
             os_.at[at], or_.at[at], device_id={"qset": to},
         )
 
@@ -326,10 +406,17 @@
             to = lax.rem(g + i, groups)
             merge(own, to, osend.at[own, to], lsend.at[own, to])
             lse_copy(own, i, False).start()
-            out_copy(own, i, False).start()
+            out_copy(own, 0, i, False).start()
             return n
 
         lax.fori_loop(0, groups - 1, one, 0)
+        for cut in range(1, PARTS):
+
+            def rest(k, n):
+                out_copy(own, cut, alternate(k, groups), False).start()
+                return n
+
+            lax.fori_loop(0, groups - 1, rest, 0)
 
     for own in range(mine):
         merge_and_send(own)
@@ -338,75 +425,72 @@
         merge(own, g, orecv.at[own, g], lrecv.at[own, g])
     lax.fori_loop(0, shards, lambda i, n: (wo_load(i).wait(), n)[1], 0)
 
-    def pair_copy(own):
+    def pair_copy(piece):
         return pltpu.make_async_remote_copy(
-            psend.at[own], precv.at[own], ps.at[own], pr.at[own], device_id={"seq": partner}
+            psend.at[piece], precv.at[piece], ps.at[piece], pr.at[piece],
+            device_id={"seq": partner},
         )
 
     def chip_part(chip):
         return pl.ds(pl.multiple_of(chip * cols, cols), cols)
 
-    def sum_copy(own, i):
+    def sum_copy(piece, i):
         to = lax.rem(x + i, chips)
-        at = own * chips + i
+        at = piece * chips + i
         return pltpu.make_async_remote_copy(
-            xsend.at[own, :, chip_part(to)], xrecv.at[own, i],
+            xsend.at[piece, :, chip_part(to)], xrecv.at[piece, i],
             xs.at[at], xr.at[at], device_id={"seq": seq_at(to, c)},
         )
 
-    def project(own):
-        def arrived(k, n):
-            i = alternate(k, groups)
-            lse_copy(own, i, True).wait_recv()
-            out_copy(own, i, True).wait_recv()
-            return n
-
-        lax.fori_loop(0, groups - 1, arrived, 0)
+    def share_of(own):
+        lax.fori_loop(
+            0, groups - 1,
+            lambda k, n: (lse_copy(own, alternate(k, groups), True).wait_recv(), n)[1], 0,
+        )
         every = lrecv[own]
         top = jnp.max(every, axis=0, keepdims=True)
         share = jnp.exp(every - top)
         share = share / jnp.sum(share, axis=0, keepdims=True)
         shares[...] = jnp.transpose(share.reshape(groups * lse_rows, LANES))
+
+    def project(own, cut):
+        piece = own * PARTS + cut
+        here = slice(cut * short, (cut + 1) * short)
+        lax.fori_loop(
+            0, groups - 1,
+            lambda k, n: (out_copy(own, cut, alternate(k, groups), True).wait_recv(), n)[1], 0,
+        )
         for j in range(pairs):
             at = slice(j * LANES, (j + 1) * LANES)
-            mixed = jnp.zeros((tokens, LANES), F32)
+            mixed = jnp.zeros((short, LANES), F32)
             for source in range(groups):
                 even, odd = source * lse_rows + j, source * lse_rows + odd_row + j
-                scale = jnp.where(
-                    low, shares[:tokens, even : even + 1], shares[:tokens, odd : odd + 1]
-                )
-                mixed = mixed + scale * orecv[own, source, :, at].astype(F32)
+                scale = jnp.where(low, shares[here, even : even + 1], shares[here, odd : odd + 1])
+                mixed = mixed + scale * orecv[own, source, here, at].astype(F32)
             att[:, at] = mixed.astype(BF16)
 
-        psend[own] = jnp.dot(att[...], wo[other], preferred_element_type=F32).astype(BF16)
-        pair_copy(own).start()
+        psend[piece] = jnp.dot(att[...], wo[other], preferred_element_type=F32).astype(BF16)
+        pair_copy(piece).start()
         half[...] = jnp.dot(att[...], wo[c], preferred_element_type=F32)
-        pair_copy(own).wait_recv()
+        pair_copy(piece).wait_recv()
 
         def add(i):
             at = chip_part(lax.rem(x + i, chips))
-            xsend[own, :, at] = (half[:, at] + precv[own, :, at].astype(F32)).astype(BF16)
+            xsend[piece, :, at] = (half[:, at] + precv[piece, :, at].astype(F32)).astype(BF16)
 
         def to_chip(k, n):
             i = alternate(k, chips)
             add(i)
-            sum_copy(own, i).start()
+            sum_copy(piece, i).start()
             return n
 
         lax.fori_loop(0, chips - 1, to_chip, 0)
         add(0)
 
     for own in range(mine):
-        project(own)
-
-    feature = pl.ds(pl.multiple_of(me * cols, cols), cols)
-    for own in range(mine):
-        here = slice(own * tokens, (own + 1) * tokens)
-        result = dec_raw[here, feature].astype(F32) + xsend[own, :, chip_part(x)].astype(F32)
-        for i in range(1, chips):
-            sum_copy(own, i).wait_recv()
-            result = result + xrecv[own, i].astype(F32)
-        out_ref[own] = result.astype(BF16)
+        share_of(own)
+        for cut in range(PARTS):
+            project(own, cut)
 
     def sent(m, n):
         right_copy(m, 0).wait_send()
@@ -422,13 +506,25 @@
     for own in range(mine):
 
         def sent_qset(i, n):
-            out_copy(own, i, False).wait_send()
             lse_copy(own, i, False).wait_send()
+            for cut in range(PARTS):
+                out_copy(own, cut, i, False).wait_send()
             return n
 
         lax.fori_loop(1, groups, sent_qset, 0)
-        pair_copy(own).wait_send()
-        lax.fori_loop(1, chips, lambda i, n: (sum_copy(own, i).wait_send(), n)[1], 0)
+
+    feature = pl.ds(pl.multiple_of(me * cols, cols), cols)
+    for piece in range(mine * PARTS):
+        here = slice(piece * short, (piece + 1) * short)
+        result = dec_raw[here, feature].astype(F32) + xsend[piece, :, chip_part(x)].astype(F32)
+        for i in range(1, chips):
+            sum_copy(piece, i).wait_recv()
+            result = result + xrecv[piece, i].astype(F32)
+        own, cut = divmod(piece, PARTS)
+        out_ref[own, cut * short : (cut + 1) * short, :] = result.astype(BF16)
+    for piece in range(mine * PARTS):
+        pair_copy(piece).wait_send()
+        lax.fori_loop(1, chips, lambda i, n: (sum_copy(piece, i).wait_send(), n)[1], 0)
 
 
 def body(
@@ -441,6 +537,7 @@
     cols = query_weight.shape[1]
     questions = mine * groups
     messages = (chips - 1) * CHUNKS // 2
+    pieces, short = mine * PARTS, tokens // PARTS
     hbm = pl.BlockSpec(memory_space=pl.ANY)
     vmem = pl.BlockSpec(memory_space=pltpu.VMEM)
     smem = pl.BlockSpec(memory_space=pltpu.SMEM)
@@ -469,12 +566,12 @@
             pltpu.VMEM((mine, groups, 8, LANES), F32),
             pltpu.VMEM((mine, groups, 8, LANES), F32),
             pltpu.VMEM((LANES, groups * 8), F32),
-            pltpu.VMEM((tokens, cols), BF16),
-            pltpu.VMEM((tokens, chips * cols), F32),
-            pltpu.VMEM((mine, tokens, chips * cols), BF16),
-            pltpu.VMEM((mine, tokens, chips * cols), BF16),
-            pltpu.VMEM((mine, tokens, chips * cols), BF16),
-            pltpu.VMEM((mine, chips, tokens, cols), BF16),
+            pltpu.VMEM((short, cols), BF16),
+            pltpu.VMEM((short, chips * cols), F32),
+            pltpu.VMEM((pieces, short, chips * cols), BF16),
+            pltpu.VMEM((pieces, short, chips * cols), BF16),
+            pltpu.VMEM((pieces, short, chips * cols), BF16),
+            pltpu.VMEM((pieces, chips, short, cols), BF16),
             pltpu.VMEM((16, width), F32),
             pltpu.SMEM((questions,), jnp.int32),
             pltpu.SMEM((questions,), jnp.int32),
@@ -483,8 +580,8 @@
             dma(messages), dma(messages), dma(messages), dma(messages),
             dma(CHUNKS * chips), dma(CHUNKS * chips),
             dma(groups), dma(groups),
-            dma(mine * groups), dma(mine * groups), dma(mine * groups), dma(mine * groups),
-            dma(mine), dma(mine), dma(mine * chips), dma(mine * chips),
+            dma(pieces * groups), dma(pieces * groups), dma(mine * groups), dma(mine * groups),
+            dma(pieces), dma(pieces), dma(pieces * chips), dma(pieces * chips),
             pltpu.SemaphoreType.REGULAR, pltpu.SemaphoreType.REGULAR,
         ],
         compiler_params=pltpu.CompilerParams(

time: 141 us -> 130 us (0.922)
  Pallas kernels: 139 us -> 128 us
    pallas_call x1, Pallas kernels: 139 us -> 128 us  [body(): pl.pallas_call(kernel, out_shape=jax.ShapeDtypeStruct((mine, tokens, cols...]
where the time goes in v3:
time: 130 us; the launch traced here: 129 us
  Pallas kernels  128 us (98%)
  local copies, waits for them, and re-layouts  1.47 us (1%)
    pallas_call x1, Pallas kernels, body(): pl.pallas_call(kernel, out_shape=jax.ShapeDtypeStruct((mine, tokens, cols...  128 us

profile of v3, /device:TPU:513, one launch (start us, length us, event | category | flops | bytes accessed | tf_op | source)
XLA Modules:
  0.0 129.5 jit_solution(18048137823731984805)
XLA Ops:
  0.0 128.0 %reader_step.1 = bf16[2,64,256]{2,1,0:T(8,128)(2,1)} custom-call(s32[8,16]{1,0:T(8,128)} %bitcast.5, bf16[128,4096]{1,0:T(8,128)(2,1)} %bitcast.3, bf16[4096]{0:T(1024)(128)(2,1)} %enc_gain.1, bf16[128,4096]{1,0:T(8,128)(2,1)} %bitcast.4, bf16[4096]{0:T(1024)(128)(2,1)} %dec_gain.1, bf16[4096,256]{1,0:T(8,128)(2,1)} %wq_hbm.1, ...), custom_call_target="tpu_custom_call" | custom-call | tf_op jit(solution)/shard_map/reader_step/pallas_call | solution.py:545
  128.0 1.5 %copy.10 = bf16[2,64,256]{2,1,0:T(8,128)(2,1)} copy(bf16[2,64,256]{2,1,0:T(8,128)(2,1)} %reader_step.1) | data formatting | bytes 131072

commit v4 on v3

--- a/solution.py
+++ b/solution.py
@@ -19,25 +19,25 @@
 BF16 = jnp.bfloat16
 
 
-def normalise(src, gain, dst_at, total_rows):
+def normalise(src, gain, dst_at, start, rows_here):
     step = 16
 
     def one(i, carry):
-        at = pl.ds(pl.multiple_of(i * step, step), step)
+        at = pl.ds(pl.multiple_of(start + i * step, step), step)
         rows = src[at, :].astype(F32)
         mean_square = jnp.mean(rows * rows, axis=-1, keepdims=True)
         dst_at[at, :] = (rows * lax.rsqrt(mean_square + EPSILON) * gain[...]).astype(BF16)
         return carry
 
-    lax.fori_loop(0, total_rows // step, one, 0)
+    lax.fori_loop(0, rows_here // step, one, 0)
 
 
 def kernel(
-    table, states_hbm, enc_gain, dec_hbm, dec_gain, wq_hbm, wkv_hbm, wo_hbm, out_ref,
+    table_hbm, states_hbm, enc_gain_hbm, dec_hbm, dec_gain_hbm, wq_hbm, wkv_hbm, wo_hbm, out_ref,
     raw, dec_raw, dec_rows, rows, wq, wkv_in, wkv, wo, kv, qbuf, num, peak, total,
     osend, orecv, lsend, lrecv, shares, att, half, psend, precv, xsend, xrecv, gains,
-    first, second, hits,
-    load_sem, rs, rr, ls, lr, ds, dr, qs, qr, os_, or_, ss, sr, ps, pr, xs, xr, rising, falling,
+    enc_gain, dec_gain, table, first, second, hits,
+    load_sem, rs, rr, lr, ds, dr, qs, qr, os_, or_, ss, sr, ps, pr, xs, xr, rising, falling,
 ):
     shards, groups = lax.axis_size("seq"), lax.axis_size("qset")
     chips = shards // CORES
@@ -59,18 +59,27 @@
     def load(i, src, dst):
         return pltpu.make_async_copy(src, dst, load_sem.at[i])
 
-    states_load = load(0, states_hbm, raw)
-    dec_load = load(1, dec_hbm, dec_raw)
-    wq_load = load(2, wq_hbm, wq)
-    wkv_load = load(3, wkv_hbm, wkv_in)
+    def states_load(k):
+        at = pl.ds(k * piece, piece)
+        return load(k, states_hbm.at[at], raw.at[at])
+
+    enc_gain_load = load(CHUNKS, enc_gain_hbm, enc_gain)
+    dec_load = load(CHUNKS + 1, dec_hbm, dec_raw)
+    wq_load = load(CHUNKS + 2, wq_hbm, wq)
+    wkv_load = load(CHUNKS + 3, wkv_hbm, wkv_in)
+    dec_gain_load = load(CHUNKS + 4, dec_gain_hbm, dec_gain)
+    table_load = load(CHUNKS + 5, table_hbm, table)
 
     def wo_load(i):
         chip, core = lax.div(i, CORES), lax.rem(i, CORES)
         src = wo_hbm.at[:, pl.ds(pl.multiple_of(i * cols, cols), cols)]
         dst = wo.at[core, :, pl.ds(pl.multiple_of(chip * cols, cols), cols)]
-        return load(4 + i, src, dst)
-
-    states_load.start()
+        return load(CHUNKS + 6, src, dst)
+
+    inward = [k // 2 if k % 2 == 0 else CHUNKS - 1 - k // 2 for k in range(CHUNKS)]
+    enc_gain_load.start()
+    for k in inward:
+        states_load(k).start()
 
     barrier = pltpu.get_barrier_semaphore()
     above, below = g + 1, g - 1
@@ -90,30 +99,20 @@
 
     if_below(lambda: pl.semaphore_signal(barrier, inc=1, device_id={"qset": below}))
 
-    gains[0:1, :] = enc_gain[...].astype(F32).reshape(1, width)
-    gains[8:9, :] = dec_gain[...].astype(F32).reshape(1, width)
-    states_load.wait()
-    dec_load.start()
-    wq_load.start()
-    wkv_load.start()
-    lax.fori_loop(0, shards, lambda i, n: (wo_load(i).start(), n)[1], 0)
-    normalise(raw, gains.at[0:1, :], rows.at[me], plen)
-    pl.semaphore_wait(barrier, 2 + (1 - c) + 1 - lax.div(g + 1, groups))
-
     def part(slot, chunk):
         return rows.at[slot, pl.ds(pl.multiple_of(chunk * piece, piece), piece), :]
 
     def right_copy(m, behind):
         at = part(seq_at(x - lax.div(m, CHUNKS) - behind, c), lax.rem(m, CHUNKS))
-        return pltpu.make_async_remote_copy(at, at, rs.at[m], rr.at[m], device_id={"seq": right})
+        return pltpu.make_async_remote_copy(at, at, rs, rr.at[m], device_id={"seq": right})
 
     def left_copy(m, behind):
         at = part(seq_at(x + lax.div(m, CHUNKS) + behind, c), CHUNKS - 1 - lax.rem(m, CHUNKS))
-        return pltpu.make_async_remote_copy(at, at, ls.at[m], lr.at[m], device_id={"seq": left})
+        return pltpu.make_async_remote_copy(at, at, rs, lr.at[m], device_id={"seq": left})
 
     def die_copy(k, slot, chunk):
         at = part(slot, chunk)
-        return pltpu.make_async_remote_copy(at, at, ds.at[k], dr.at[k], device_id={"seq": partner})
+        return pltpu.make_async_remote_copy(at, at, ds, dr.at[k], device_id={"seq": partner})
 
     def from_left(m, core):
         return seq_at(x - lax.div(m, CHUNKS) - 1, core), lax.rem(m, CHUNKS)
@@ -121,17 +120,28 @@
     def from_right(m, core):
         return seq_at(x + lax.div(m, CHUNKS) + 1, core), CHUNKS - 1 - lax.rem(m, CHUNKS)
 
-    def start_own(m, n):
-        right_copy(m, 0).start()
-        left_copy(m, 0).start()
-
-        @pl.when(c == 0)
-        def _():
-            die_copy(m, me, m).start()
-
-        return n
-
-    lax.fori_loop(0, CHUNKS, start_own, 0)
+    enc_gain_load.wait()
+    gains[0:1, :] = enc_gain[...].astype(F32).reshape(1, width)
+    done, sent_right, sent_left = set(), 0, 0
+    for k in inward:
+        states_load(k).wait()
+        normalise(raw, gains.at[0:1, :], rows.at[me], k * piece, piece)
+        if not done:
+            pl.semaphore_wait(barrier, 2 + (1 - c) + 1 - lax.div(g + 1, groups))
+        done.add(k)
+        while sent_right in done:
+            right_copy(jnp.int32(sent_right), 0).start()
+            sent_right += 1
+        while CHUNKS - 1 - sent_left in done:
+            left_copy(jnp.int32(sent_left), 0).start()
+            sent_left += 1
+    for one in (wkv_load, dec_load, dec_gain_load, wq_load, table_load):
+        one.start()
+    lax.fori_loop(0, shards, lambda i, n: (wo_load(i).start(), n)[1], 0)
+
+    @pl.when(c == 0)
+    def _():
+        lax.fori_loop(0, CHUNKS, lambda m, n: (die_copy(m, me, m).start(), n)[1], 0)
 
     @pl.when(g == 0)
     def _():
@@ -141,7 +151,9 @@
 
     def own_queries():
         dec_load.wait()
-        normalise(dec_raw, gains.at[8:9, :], dec_rows, dec_raw.shape[0])
+        dec_gain_load.wait()
+        gains[8:9, :] = dec_gain[...].astype(F32).reshape(1, width)
+        normalise(dec_raw, gains.at[8:9, :], dec_rows, 0, dec_raw.shape[0])
         wq_load.wait()
         queries = jnp.dot(dec_rows[...], wq[...], preferred_element_type=F32).astype(BF16)
         own_q[...] = queries.reshape(mine, tokens, cols)
@@ -149,12 +161,12 @@
     def query_copy(i):
         to = lax.rem(g + i, groups)
         return pltpu.make_async_remote_copy(
-            own_q, own_q, qs.at[i], qr.at[i], device_id={"qset": to}
+            own_q, own_q, qs, qr, device_id={"qset": to}
         )
 
-    def query_arrival(i):
-        at = qbuf.at[pl.ds(lax.rem(g - i + groups, groups) * mine, mine)]
-        return pltpu.make_async_remote_copy(at, at, qs.at[i], qr.at[i], device_id={"qset": g})
+    def query_all():
+        at = qbuf.at[pl.ds(0, questions - mine)]
+        return pltpu.make_async_remote_copy(at, at, qs, qr, device_id={"qset": above})
 
     passages = table.shape[1]
 
@@ -292,6 +304,7 @@
 
         @pl.when(m == hold + 1)
         def _():
+            table_load.wait()
             lax.fori_loop(0, questions, find, 0)
 
         @pl.when(m == partner_at)
@@ -325,7 +338,7 @@
 
         @pl.when(m == messages // 2)
         def _():
-            lax.fori_loop(1, groups, lambda i, k: (query_arrival(i).wait_recv(), k)[1], 0)
+            query_all().wait_recv()
             lax.fori_loop(0, CORES, lambda i, k: (attend(seq_at(x, i)), k)[1], 0)
 
         for far in range(1, chips // 2):
@@ -356,26 +369,32 @@
 
     short = tokens // PARTS
 
-    def out_copy(own, cut, i, arrival):
+    def out_copy(own, cut, i):
         to = lax.rem(g + i, groups)
-        source = lax.rem(g - i + groups, groups)
-        at = (own * PARTS + cut) * groups + i
         here = pl.ds(cut * short, short)
         return pltpu.make_async_remote_copy(
             osend.at[own, to, here],
-            orecv.at[own, source if arrival else g, here],
-            os_.at[at], or_.at[at], device_id={"qset": to},
+            orecv.at[own, g, here],
+            os_, or_.at[own * PARTS + cut], device_id={"qset": to},
         )
 
-    def lse_copy(own, i, arrival):
+    def out_all(own, cut):
+        at = orecv.at[own, pl.ds(0, groups - 1), pl.ds(cut * short, short)]
+        return pltpu.make_async_remote_copy(
+            at, at, os_, or_.at[own * PARTS + cut], device_id={"qset": above}
+        )
+
+    def lse_copy(own, i):
         to = lax.rem(g + i, groups)
-        source = lax.rem(g - i + groups, groups)
-        at = own * groups + i
         return pltpu.make_async_remote_copy(
             lsend.at[own, to],
-            lrecv.at[own, source if arrival else g],
-            ss.at[at], sr.at[at], device_id={"qset": to},
+            lrecv.at[own, g],
+            ss, sr.at[own], device_id={"qset": to},
         )
+
+    def lse_all(own):
+        at = lrecv.at[own, pl.ds(0, groups - 1)]
+        return pltpu.make_async_remote_copy(at, at, ss, sr.at[own], device_id={"qset": above})
 
     def merge(own, to, mix_at, lse_at):
         q = to * mine + own
@@ -405,15 +424,15 @@
             i = alternate(k, groups)
             to = lax.rem(g + i, groups)
             merge(own, to, osend.at[own, to], lsend.at[own, to])
-            lse_copy(own, i, False).start()
-            out_copy(own, 0, i, False).start()
+            lse_copy(own, i).start()
+            out_copy(own, 0, i).start()
             return n
 
         lax.fori_loop(0, groups - 1, one, 0)
         for cut in range(1, PARTS):
 
             def rest(k, n):
-                out_copy(own, cut, alternate(k, groups), False).start()
+                out_copy(own, cut, alternate(k, groups)).start()
                 return n
 
             lax.fori_loop(0, groups - 1, rest, 0)
@@ -423,11 +442,11 @@
     for own in range(mine):
         lrecv[own, g] = lrecv_pad
         merge(own, g, orecv.at[own, g], lrecv.at[own, g])
-    lax.fori_loop(0, shards, lambda i, n: (wo_load(i).wait(), n)[1], 0)
+    pltpu.make_async_copy(wo, wo, load_sem.at[CHUNKS + 6]).wait()
 
     def pair_copy(piece):
         return pltpu.make_async_remote_copy(
-            psend.at[piece], precv.at[piece], ps.at[piece], pr.at[piece],
+            psend.at[piece], precv.at[piece], ps, pr.at[piece],
             device_id={"seq": partner},
         )
 
@@ -436,17 +455,17 @@
 
     def sum_copy(piece, i):
         to = lax.rem(x + i, chips)
-        at = piece * chips + i
         return pltpu.make_async_remote_copy(
             xsend.at[piece, :, chip_part(to)], xrecv.at[piece, i],
-            xs.at[at], xr.at[at], device_id={"seq": seq_at(to, c)},
+            xs, xr.at[piece], device_id={"seq": seq_at(to, c)},
         )
 
+    def sum_all(piece):
+        at = xrecv.at[piece, pl.ds(1, chips - 1)]
+        return pltpu.make_async_remote_copy(at, at, xs, xr.at[piece], device_id={"seq": right})
+
     def share_of(own):
-        lax.fori_loop(
-            0, groups - 1,
-            lambda k, n: (lse_copy(own, alternate(k, groups), True).wait_recv(), n)[1], 0,
-        )
+        lse_all(own).wait_recv()
         every = lrecv[own]
         top = jnp.max(every, axis=0, keepdims=True)
         share = jnp.exp(every - top)
@@ -456,10 +475,7 @@
     def project(own, cut):
         piece = own * PARTS + cut
         here = slice(cut * short, (cut + 1) * short)
-        lax.fori_loop(
-            0, groups - 1,
-            lambda k, n: (out_copy(own, cut, alternate(k, groups), True).wait_recv(), n)[1], 0,
-        )
+        out_all(own, cut).wait_recv()
         for j in range(pairs):
             at = slice(j * LANES, (j + 1) * LANES)
             mixed = jnp.zeros((short, LANES), F32)
@@ -492,39 +508,27 @@
         for cut in range(PARTS):
             project(own, cut)
 
-    def sent(m, n):
-        right_copy(m, 0).wait_send()
-        left_copy(m, 0).wait_send()
-        return n
-
-    lax.fori_loop(0, messages, sent, 0)
-    lax.fori_loop(
-        0, CHUNKS * chips, lambda k, n: (die_copy(k, me, 0).wait_send(), n)[1], 0
-    )
-
-    lax.fori_loop(1, groups, lambda i, n: (query_copy(i).wait_send(), n)[1], 0)
-    for own in range(mine):
-
-        def sent_qset(i, n):
-            lse_copy(own, i, False).wait_send()
-            for cut in range(PARTS):
-                out_copy(own, cut, i, False).wait_send()
-            return n
-
-        lax.fori_loop(1, groups, sent_qset, 0)
-
+    def sent(all_of, sem):
+        pltpu.make_async_remote_copy(
+            all_of, all_of, sem, qr, device_id={"seq": right}
+        ).wait_send()
+
+    sent(rows.at[pl.ds(0, chips - 1)], rs)
+    sent(rows.at[pl.ds(0, chips)], ds)
+    sent(qbuf.at[pl.ds(0, questions - mine)], qs)
+    sent(osend.at[:, pl.ds(0, groups - 1)], os_)
+    sent(lsend.at[:, pl.ds(0, groups - 1)], ss)
     feature = pl.ds(pl.multiple_of(me * cols, cols), cols)
     for piece in range(mine * PARTS):
         here = slice(piece * short, (piece + 1) * short)
         result = dec_raw[here, feature].astype(F32) + xsend[piece, :, chip_part(x)].astype(F32)
+        sum_all(piece).wait_recv()
         for i in range(1, chips):
-            sum_copy(piece, i).wait_recv()
             result = result + xrecv[piece, i].astype(F32)
         own, cut = divmod(piece, PARTS)
         out_ref[own, cut * short : (cut + 1) * short, :] = result.astype(BF16)
-    for piece in range(mine * PARTS):
-        pair_copy(piece).wait_send()
-        lax.fori_loop(1, chips, lambda i, n: (sum_copy(piece, i).wait_send(), n)[1], 0)
+    sent(psend, ps)
+    sent(xrecv.at[:, pl.ds(0, chips - 1)], xs)
 
 
 def body(
@@ -540,12 +544,12 @@
     pieces, short = mine * PARTS, tokens // PARTS
     hbm = pl.BlockSpec(memory_space=pl.ANY)
     vmem = pl.BlockSpec(memory_space=pltpu.VMEM)
-    smem = pl.BlockSpec(memory_space=pltpu.SMEM)
     dma = lambda n: pltpu.SemaphoreType.DMA((n,))
+    one = pltpu.SemaphoreType.DMA
     return pl.pallas_call(
         kernel,
         out_shape=jax.ShapeDtypeStruct((mine, tokens, cols), BF16),
-        in_specs=[smem, hbm, vmem, hbm, vmem, hbm, hbm, hbm],
+        in_specs=[hbm] * 8,
         out_specs=vmem,
         scratch_shapes=[
             pltpu.VMEM((plen, width), BF16),
@@ -573,15 +577,17 @@
             pltpu.VMEM((pieces, short, chips * cols), BF16),
             pltpu.VMEM((pieces, chips, short, cols), BF16),
             pltpu.VMEM((16, width), F32),
+            pltpu.VMEM((width,), BF16),
+            pltpu.VMEM((width,), BF16),
+            pltpu.SMEM(question_of.shape[:2], jnp.int32),
             pltpu.SMEM((questions,), jnp.int32),
             pltpu.SMEM((questions,), jnp.int32),
             pltpu.SMEM((questions,), jnp.int32),
-            dma(4 + shards),
-            dma(messages), dma(messages), dma(messages), dma(messages),
-            dma(CHUNKS * chips), dma(CHUNKS * chips),
-            dma(groups), dma(groups),
-            dma(pieces * groups), dma(pieces * groups), dma(mine * groups), dma(mine * groups),
-            dma(pieces), dma(pieces), dma(pieces * chips), dma(pieces * chips),
+            dma(CHUNKS + 7),
+            one, dma(messages), dma(messages),
+            one, dma(CHUNKS * chips),
+            one, one, one, dma(pieces), one, dma(mine),
+            one, dma(pieces), one, dma(pieces),
             pltpu.SemaphoreType.REGULAR, pltpu.SemaphoreType.REGULAR,
         ],
         compiler_params=pltpu.CompilerParams(

time: 130 us -> 126 us (0.969)
  Pallas kernels: 128 us -> 124 us
    pallas_call x1, Pallas kernels: 128 us -> 124 us  [body(): pl.pallas_call(kernel, out_shape=jax.ShapeDtypeStruct((mine, tokens, cols...]
where the time goes in v4:
time: 126 us
  Pallas kernels  124 us (98%)
  local copies, waits for them, and re-layouts  1.47 us (1%)
    pallas_call x1, Pallas kernels, body(): pl.pallas_call(kernel, out_shape=jax.ShapeDtypeStruct((mine, tokens, cols...  124 us

profile of v4, /device:TPU:513, one launch (start us, length us, event | category | flops | bytes accessed | tf_op | source)
XLA Modules:
  0.0 125.9 jit_solution(6374648383860581188)
XLA Ops:
  0.0 124.4 %reader_step.1 = bf16[2,64,256]{2,1,0:T(8,128)(2,1)} custom-call(s32[8,16]{1,0:T(8,128)} %bitcast.5, bf16[128,4096]{1,0:T(8,128)(2,1)} %bitcast.3, bf16[4096]{0:T(1024)(128)(2,1)} %enc_gain_hbm.1, bf16[128,4096]{1,0:T(8,128)(2,1)} %bitcast.4, bf16[4096]{0:T(1024)(128)(2,1)} %dec_gain_hbm.1, bf16[4096,256]{1,0:T(8,128)(2,1)} %wq_hbm.1, ...), custom_call_target="tpu_custom_call" | custom-call | tf_op jit(solution)/shard_map/reader_step/pallas_call | solution.py:549
  124.4 1.5 %copy.10 = bf16[2,64,256]{2,1,0:T(8,128)(2,1)} copy(bf16[2,64,256]{2,1,0:T(8,128)(2,1)} %reader_step.1) | data formatting | bytes 131072

commit v5 on v4

--- a/solution.py
+++ b/solution.py
@@ -247,6 +247,10 @@
         return m + LAG if m + LAG < catch else max(catch, m + 1)
 
     def step(m, n):
+        @pl.when(m > catch)
+        def _():
+            partner_part(m - 1)
+
         right_copy(m, 1).wait_recv()
 
         @pl.when(m + CHUNKS < messages)
@@ -331,10 +335,6 @@
             lax.fori_loop(
                 max(0, catch - LAG), catch, lambda k, t: (partner_part(k), t)[1], 0
             )
-
-        @pl.when(m > catch)
-        def _():
-            partner_part(m - 1)
 
         @pl.when(m == messages // 2)
         def _():
@@ -355,13 +355,11 @@
         return n
 
     lax.fori_loop(0, messages, step, 0)
+    attend(seq_at(x + chips // 2, c))
     partner_part(messages - 1)
-    attend(seq_at(x + chips // 2, c))
     attend(seq_at(x + chips // 2, other))
 
     pairs = cols // LANES
-    odd_row = 4
-    lse_rows = lsend.shape[2]
 
     def alternate(k, n):
         reach = lax.div(k + 1, 2)
@@ -399,7 +397,7 @@
     def merge(own, to, mix_at, lse_at):
         q = to * mine + own
         at0, at1, count = first[q], second[q], hits[q]
-        packed = jnp.zeros((tokens, LANES), F32)
+        lses = []
         for j in range(pairs):
             at = slice(j * LANES, (j + 1) * LANES)
             top0 = jnp.where(count >= 1, peak[at0, :, at], DEAD)
@@ -412,12 +410,9 @@
             mix = (scale0 * num[at0, :, at] + scale1 * num[at1, :, at]) / mass
             mix_at[:, at] = mix.astype(BF16)
             lse = jnp.where(count >= 1, top + jnp.log(mass), DEAD)
-            packed = jnp.where((lane == j) | (lane == HD + odd_row + j), lse, packed)
-        turned = jnp.transpose(packed)
-        lse_at[:, :tokens] = turned[:lse_rows] + turned[HD : HD + lse_rows]
-
-    lsend[...] = jnp.zeros_like(lsend)
-    lrecv_pad = jnp.zeros(lrecv.shape[2:], F32)
+            turned = jnp.transpose(lse)
+            lses += [turned[:1], turned[HD : HD + 1]]
+        lse_at[...] = jnp.concatenate(lses, axis=1)
 
     def merge_and_send(own):
         def one(k, n):
@@ -440,7 +435,6 @@
     for own in range(mine):
         merge_and_send(own)
     for own in range(mine):
-        lrecv[own, g] = lrecv_pad
         merge(own, g, orecv.at[own, g], lrecv.at[own, g])
     pltpu.make_async_copy(wo, wo, load_sem.at[CHUNKS + 6]).wait()
 
@@ -466,22 +460,26 @@
 
     def share_of(own):
         lse_all(own).wait_recv()
-        every = lrecv[own]
+        every = jnp.concatenate([lrecv[own, k] for k in range(groups)], axis=0)
         top = jnp.max(every, axis=0, keepdims=True)
         share = jnp.exp(every - top)
         share = share / jnp.sum(share, axis=0, keepdims=True)
-        shares[...] = jnp.transpose(share.reshape(groups * lse_rows, LANES))
+        for j in range(pairs):
+            shares[j] = jnp.transpose(share[:, j * LANES : (j + 1) * LANES])
 
     def project(own, cut):
         piece = own * PARTS + cut
         here = slice(cut * short, (cut + 1) * short)
+        odd_here = slice(HD + cut * short, HD + (cut + 1) * short)
         out_all(own, cut).wait_recv()
         for j in range(pairs):
             at = slice(j * LANES, (j + 1) * LANES)
             mixed = jnp.zeros((short, LANES), F32)
             for source in range(groups):
-                even, odd = source * lse_rows + j, source * lse_rows + odd_row + j
-                scale = jnp.where(low, shares[here, even : even + 1], shares[here, odd : odd + 1])
+                at_source = slice(source, source + 1)
+                scale = jnp.where(
+                    low, shares[j, here, at_source], shares[j, odd_here, at_source]
+                )
                 mixed = mixed + scale * orecv[own, source, here, at].astype(F32)
             att[:, at] = mixed.astype(BF16)
 
@@ -567,9 +565,9 @@
             pltpu.VMEM((shards, tokens, cols), F32),
             pltpu.VMEM((mine, groups, tokens, cols), BF16),
             pltpu.VMEM((mine, groups, tokens, cols), BF16),
-            pltpu.VMEM((mine, groups, 8, LANES), F32),
-            pltpu.VMEM((mine, groups, 8, LANES), F32),
-            pltpu.VMEM((LANES, groups * 8), F32),
+            pltpu.VMEM((mine, groups, 1, tokens * cols // HD), F32),
+            pltpu.VMEM((mine, groups, 1, tokens * cols // HD), F32),
+            pltpu.VMEM((cols // LANES, LANES, groups), F32),
             pltpu.VMEM((short, cols), BF16),
             pltpu.VMEM((short, chips * cols), F32),
             pltpu.VMEM((pieces, short, chips * cols), BF16),

time: 126 us -> 125 us (level)
    pallas_call x1, Pallas kernels: 124 us -> 123 us  [body(): pl.pallas_call(kernel, out_shape=jax.ShapeDtypeStruct((mine, tokens, cols...]
where the time goes in v5:
time: 125 us; the launch traced here: 124 us
  Pallas kernels  123 us (98%)
  local copies, waits for them, and re-layouts  1.47 us (1%)
    pallas_call x1, Pallas kernels, body(): pl.pallas_call(kernel, out_shape=jax.ShapeDtypeStruct((mine, tokens, cols...  123 us

profile of v5, /device:TPU:513, one launch (start us, length us, event | category | flops | bytes accessed | tf_op | source)
XLA Modules:
  0.0 124.4 jit_solution(1915852629584229599)
XLA Ops:
  0.0 122.9 %reader_step.1 = bf16[2,64,256]{2,1,0:T(8,128)(2,1)} custom-call(s32[8,16]{1,0:T(8,128)} %bitcast.5, bf16[128,4096]{1,0:T(8,128)(2,1)} %bitcast.3, bf16[4096]{0:T(1024)(128)(2,1)} %enc_gain_hbm.1, bf16[128,4096]{1,0:T(8,128)(2,1)} %bitcast.4, bf16[4096]{0:T(1024)(128)(2,1)} %dec_gain_hbm.1, bf16[4096,256]{1,0:T(8,128)(2,1)} %wq_hbm.1, ...), custom_call_target="tpu_custom_call" | custom-call | tf_op jit(solution)/shard_map/reader_step/pallas_call | solution.py:547
  122.9 1.5 %copy.10 = bf16[2,64,256]{2,1,0:T(8,128)(2,1)} copy(bf16[2,64,256]{2,1,0:T(8,128)(2,1)} %reader_step.1) | data formatting | bytes 131072

commit v6 on v5

--- a/solution.py
+++ b/solution.py
@@ -14,9 +14,14 @@
 CORES = 2
 CHUNKS = 4
 LAG = 4
-PARTS = 2
 F32 = jnp.float32
 BF16 = jnp.bfloat16
+
+
+def pieces_of(mine, tokens):
+    half, quarter = tokens // 2, tokens // 4
+    pieces = [(own, start, half) for own in range(mine) for start in (0, half)]
+    return pieces[:-1] + [(mine - 1, half, quarter), (mine - 1, half + quarter, quarter)]
 
 
 def normalise(src, gain, dst_at, start, rows_here):
@@ -33,9 +38,9 @@
 
 
 def kernel(
-    table_hbm, states_hbm, enc_gain_hbm, dec_hbm, dec_gain_hbm, wq_hbm, wkv_hbm, wo_hbm, out_ref,
+    table_hbm, states_hbm, enc_gain_hbm, dec_hbm, dec_gain_hbm, wq_hbm, wkv_hbm, wo_hbm, out_hbm,
     raw, dec_raw, dec_rows, rows, wq, wkv_in, wkv, wo, kv, qbuf, num, peak, total,
-    osend, orecv, lsend, lrecv, shares, att, half, psend, precv, xsend, xrecv, gains,
+    osend, orecv, lsend, lrecv, shares, att, half, psend, precv, xsend, xrecv, out_here, gains,
     enc_gain, dec_gain, table, first, second, hits,
     load_sem, rs, rr, lr, ds, dr, qs, qr, os_, or_, ss, sr, ps, pr, xs, xr, rising, falling,
 ):
@@ -365,22 +370,22 @@
         reach = lax.div(k + 1, 2)
         return n // 2 - reach + 2 * reach * lax.rem(k, 2)
 
-    short = tokens // PARTS
-
-    def out_copy(own, cut, i):
+    pieces = pieces_of(mine, tokens)
+
+    def out_copy(p, i):
+        own, start, size = pieces[p]
         to = lax.rem(g + i, groups)
-        here = pl.ds(cut * short, short)
+        here = pl.ds(start, size)
         return pltpu.make_async_remote_copy(
             osend.at[own, to, here],
             orecv.at[own, g, here],
-            os_, or_.at[own * PARTS + cut], device_id={"qset": to},
+            os_, or_.at[p], device_id={"qset": to},
         )
 
-    def out_all(own, cut):
-        at = orecv.at[own, pl.ds(0, groups - 1), pl.ds(cut * short, short)]
-        return pltpu.make_async_remote_copy(
-            at, at, os_, or_.at[own * PARTS + cut], device_id={"qset": above}
-        )
+    def out_all(p):
+        own, start, size = pieces[p]
+        at = orecv.at[own, pl.ds(0, groups - 1), pl.ds(start, size)]
+        return pltpu.make_async_remote_copy(at, at, os_, or_.at[p], device_id={"qset": above})
 
     def lse_copy(own, i):
         to = lax.rem(g + i, groups)
@@ -415,19 +420,21 @@
         lse_at[...] = jnp.concatenate(lses, axis=1)
 
     def merge_and_send(own):
+        lead, *others = [p for p in range(len(pieces)) if pieces[p][0] == own]
+
         def one(k, n):
             i = alternate(k, groups)
             to = lax.rem(g + i, groups)
             merge(own, to, osend.at[own, to], lsend.at[own, to])
             lse_copy(own, i).start()
-            out_copy(own, 0, i).start()
+            out_copy(lead, i).start()
             return n
 
         lax.fori_loop(0, groups - 1, one, 0)
-        for cut in range(1, PARTS):
+        for p in others:
 
             def rest(k, n):
-                out_copy(own, cut, alternate(k, groups)).start()
+                out_copy(p, alternate(k, groups)).start()
                 return n
 
             lax.fori_loop(0, groups - 1, rest, 0)
@@ -438,25 +445,29 @@
         merge(own, g, orecv.at[own, g], lrecv.at[own, g])
     pltpu.make_async_copy(wo, wo, load_sem.at[CHUNKS + 6]).wait()
 
-    def pair_copy(piece):
+    def rows_of(p):
+        own, start, size = pieces[p]
+        return pl.ds(own * tokens + start, size)
+
+    def pair_copy(p):
+        at = rows_of(p)
         return pltpu.make_async_remote_copy(
-            psend.at[piece], precv.at[piece], ps, pr.at[piece],
-            device_id={"seq": partner},
+            psend.at[at], precv.at[at], ps, pr.at[p], device_id={"seq": partner}
         )
 
     def chip_part(chip):
         return pl.ds(pl.multiple_of(chip * cols, cols), cols)
 
-    def sum_copy(piece, i):
+    def sum_copy(p, i):
         to = lax.rem(x + i, chips)
         return pltpu.make_async_remote_copy(
-            xsend.at[piece, :, chip_part(to)], xrecv.at[piece, i],
-            xs, xr.at[piece], device_id={"seq": seq_at(to, c)},
+            xsend.at[rows_of(p), chip_part(to)], xrecv.at[i, rows_of(p)],
+            xs, xr.at[p], device_id={"seq": seq_at(to, c)},
         )
 
-    def sum_all(piece):
-        at = xrecv.at[piece, pl.ds(1, chips - 1)]
-        return pltpu.make_async_remote_copy(at, at, xs, xr.at[piece], device_id={"seq": right})
+    def sum_all(p):
+        at = xrecv.at[pl.ds(1, chips - 1), rows_of(p)]
+        return pltpu.make_async_remote_copy(at, at, xs, xr.at[p], device_id={"seq": right})
 
     def share_of(own):
         lse_all(own).wait_recv()
@@ -467,44 +478,48 @@
         for j in range(pairs):
             shares[j] = jnp.transpose(share[:, j * LANES : (j + 1) * LANES])
 
-    def project(own, cut):
-        piece = own * PARTS + cut
-        here = slice(cut * short, (cut + 1) * short)
-        odd_here = slice(HD + cut * short, HD + (cut + 1) * short)
-        out_all(own, cut).wait_recv()
+    def project(p):
+        own, start, size = pieces[p]
+        here = slice(start, start + size)
+        odd_here = slice(HD + start, HD + start + size)
+        out_all(p).wait_recv()
         for j in range(pairs):
             at = slice(j * LANES, (j + 1) * LANES)
-            mixed = jnp.zeros((short, LANES), F32)
+            mixed = jnp.zeros((size, LANES), F32)
             for source in range(groups):
                 at_source = slice(source, source + 1)
                 scale = jnp.where(
                     low, shares[j, here, at_source], shares[j, odd_here, at_source]
                 )
                 mixed = mixed + scale * orecv[own, source, here, at].astype(F32)
-            att[:, at] = mixed.astype(BF16)
-
-        psend[piece] = jnp.dot(att[...], wo[other], preferred_element_type=F32).astype(BF16)
-        pair_copy(piece).start()
-        half[...] = jnp.dot(att[...], wo[c], preferred_element_type=F32)
-        pair_copy(piece).wait_recv()
+            att[:size, at] = mixed.astype(BF16)
+
+        attended = att[:size, :]
+        psend[rows_of(p), :] = jnp.dot(
+            attended, wo[other], preferred_element_type=F32
+        ).astype(BF16)
+        pair_copy(p).start()
+        half[:size, :] = jnp.dot(attended, wo[c], preferred_element_type=F32)
+        pair_copy(p).wait_recv()
 
         def add(i):
             at = chip_part(lax.rem(x + i, chips))
-            xsend[piece, :, at] = (half[:, at] + precv[piece, :, at].astype(F32)).astype(BF16)
+            both = half[:size, at] + precv[rows_of(p), at].astype(F32)
+            xsend[rows_of(p), at] = both.astype(BF16)
 
         def to_chip(k, n):
             i = alternate(k, chips)
             add(i)
-            sum_copy(piece, i).start()
+            sum_copy(p, i).start()
             return n
 
         lax.fori_loop(0, chips - 1, to_chip, 0)
         add(0)
 
-    for own in range(mine):
-        share_of(own)
-        for cut in range(PARTS):
-            project(own, cut)
+    for p, (own, start, size) in enumerate(pieces):
+        if start == 0:
+            share_of(own)
+        project(p)
 
     def sent(all_of, sem):
         pltpu.make_async_remote_copy(
@@ -517,16 +532,24 @@
     sent(osend.at[:, pl.ds(0, groups - 1)], os_)
     sent(lsend.at[:, pl.ds(0, groups - 1)], ss)
     feature = pl.ds(pl.multiple_of(me * cols, cols), cols)
-    for piece in range(mine * PARTS):
-        here = slice(piece * short, (piece + 1) * short)
-        result = dec_raw[here, feature].astype(F32) + xsend[piece, :, chip_part(x)].astype(F32)
-        sum_all(piece).wait_recv()
+    def out_store(p):
+        own, start, size = pieces[p]
+        return pltpu.make_async_copy(
+            out_here.at[rows_of(p)], out_hbm.at[own, pl.ds(start, size)], load_sem.at[p]
+        )
+
+    for p in range(len(pieces)):
+        at = rows_of(p)
+        result = dec_raw[at, feature].astype(F32) + xsend[at, chip_part(x)].astype(F32)
+        sum_all(p).wait_recv()
         for i in range(1, chips):
-            result = result + xrecv[piece, i].astype(F32)
-        own, cut = divmod(piece, PARTS)
-        out_ref[own, cut * short : (cut + 1) * short, :] = result.astype(BF16)
+            result = result + xrecv[i, at].astype(F32)
+        out_here[at, :] = result.astype(BF16)
+        out_store(p).start()
     sent(psend, ps)
-    sent(xrecv.at[:, pl.ds(0, chips - 1)], xs)
+    sent(xrecv.at[pl.ds(0, chips - 1)], xs)
+    for p in range(len(pieces)):
+        out_store(p).wait()
 
 
 def body(
@@ -539,16 +562,15 @@
     cols = query_weight.shape[1]
     questions = mine * groups
     messages = (chips - 1) * CHUNKS // 2
-    pieces, short = mine * PARTS, tokens // PARTS
+    pieces = len(pieces_of(mine, tokens))
     hbm = pl.BlockSpec(memory_space=pl.ANY)
-    vmem = pl.BlockSpec(memory_space=pltpu.VMEM)
     dma = lambda n: pltpu.SemaphoreType.DMA((n,))
     one = pltpu.SemaphoreType.DMA
     return pl.pallas_call(
         kernel,
         out_shape=jax.ShapeDtypeStruct((mine, tokens, cols), BF16),
         in_specs=[hbm] * 8,
-        out_specs=vmem,
+        out_specs=hbm,
         scratch_shapes=[
             pltpu.VMEM((plen, width), BF16),
             pltpu.VMEM((mine * tokens, width), BF16),
@@ -568,12 +590,13 @@
             pltpu.VMEM((mine, groups, 1, tokens * cols // HD), F32),
             pltpu.VMEM((mine, groups, 1, tokens * cols // HD), F32),
             pltpu.VMEM((cols // LANES, LANES, groups), F32),
-            pltpu.VMEM((short, cols), BF16),
-            pltpu.VMEM((short, chips * cols), F32),
-            pltpu.VMEM((pieces, short, chips * cols), BF16),
-            pltpu.VMEM((pieces, short, chips * cols), BF16),
-            pltpu.VMEM((pieces, short, chips * cols), BF16),
-            pltpu.VMEM((pieces, chips, short, cols), BF16),
+            pltpu.VMEM((tokens // 2, cols), BF16),
+            pltpu.VMEM((tokens // 2, chips * cols), F32),
+            pltpu.VMEM((mine * tokens, chips * cols), BF16),
+            pltpu.VMEM((mine * tokens, chips * cols), BF16),
+            pltpu.VMEM((mine * tokens, chips * cols), BF16),
+            pltpu.VMEM((chips, mine * tokens, cols), BF16),
+            pltpu.VMEM((mine * tokens, cols), BF16),
             pltpu.VMEM((16, width), F32),
             pltpu.VMEM((width,), BF16),
             pltpu.VMEM((width,), BF16),

time: 125 us -> 125 us (level)
  no operation moved by 1% of the time
where the time goes in v6:
time: 125 us
  Pallas kernels  124 us (99%)
  local copies, waits for them, and re-layouts  1.47 us (1%)
    pallas_call x1, Pallas kernels, body(): pl.pallas_call(kernel, out_shape=jax.ShapeDtypeStruct((mine, tokens, cols...  124 us

profile of v6, /device:TPU:513, one launch (start us, length us, event | category | flops | bytes accessed | tf_op | source)
XLA Modules:
  0.0 125.0 jit_solution(15555926929174860205)
XLA Ops:
  0.0 123.5 %reader_step.1 = bf16[2,64,256]{2,1,0:T(8,128)(2,1)} custom-call(s32[8,16]{1,0:T(8,128)} %bitcast.5, bf16[128,4096]{1,0:T(8,128)(2,1)} %bitcast.3, bf16[4096]{0:T(1024)(128)(2,1)} %enc_gain_hbm.1, bf16[128,4096]{1,0:T(8,128)(2,1)} %bitcast.4, bf16[4096]{0:T(1024)(128)(2,1)} %dec_gain_hbm.1, bf16[4096,256]{1,0:T(8,128)(2,1)} %wq_hbm.1, ...), custom_call_target="tpu_custom_call" | custom-call | tf_op jit(solution)/shard_map/reader_step/pallas_call | solution.py:569
  123.5 1.5 %copy.10 = bf16[2,64,256]{2,1,0:T(8,128)(2,1)} copy(bf16[2,64,256]{2,1,0:T(8,128)(2,1)} %reader_step.1) | data formatting | bytes 131072

commit v7 on v5

--- a/solution.py
+++ b/solution.py
@@ -110,9 +110,11 @@
         at = part(seq_at(x + lax.div(m, CHUNKS) + behind, c), CHUNKS - 1 - lax.rem(m, CHUNKS))
         return pltpu.make_async_remote_copy(at, at, rs, lr.at[m], device_id={"seq": left})
 
-    def die_copy(k, slot, chunk):
-        at = part(slot, chunk)
+    def die_copy(at, k):
         return pltpu.make_async_remote_copy(at, at, ds, dr.at[k], device_id={"seq": partner})
+
+    def die_own(slot):
+        return die_copy(rows.at[slot], 0)
 
     def from_left(m, core):
         return seq_at(x - lax.div(m, CHUNKS) - 1, core), lax.rem(m, CHUNKS)
@@ -141,7 +143,7 @@
 
     @pl.when(c == 0)
     def _():
-        lax.fori_loop(0, CHUNKS, lambda m, n: (die_copy(m, me, m).start(), n)[1], 0)
+        die_own(me).start()
 
     @pl.when(g == 0)
     def _():
@@ -229,15 +231,14 @@
         kv[slot] = result.astype(BF16)
 
     def partner_part(m):
-        die_copy(CHUNKS + m, *from_left(m, other)).wait_recv()
-        die_copy(CHUNKS + messages + m, *from_right(m, other)).wait_recv()
+        die_copy(rows.at[partner, pl.ds(0, 2 * piece)], 1 + m).wait_recv()
         key_values([from_left(m, other), from_right(m, other)])
 
     def die_right(m):
-        die_copy(CHUNKS + m, *from_left(m, c)).start()
+        die_copy(part(*from_left(m, c)), 1 + m).start()
 
     def die_left(m):
-        die_copy(CHUNKS + messages + m, *from_right(m, c)).start()
+        die_copy(part(*from_right(m, c)), 1 + m).start()
 
     hold = 2
     catch = messages - 4
@@ -292,8 +293,8 @@
         def _():
             @pl.when(c == 1)
             def _():
-                die_copy(0, partner, 0).wait_recv()
-                lax.fori_loop(0, CHUNKS, lambda k, t: (die_copy(k, me, k).start(), t)[1], 0)
+                die_own(partner).wait_recv()
+                die_own(me).start()
 
                 def late(k, t):
                     die_right(k)
@@ -315,11 +316,8 @@
         def _():
             @pl.when(c == 0)
             def _():
-                die_copy(0, partner, 0).wait_recv()
-
-            lax.fori_loop(
-                1, CHUNKS, lambda k, t: (die_copy(k, partner, k).wait_recv(), t)[1], 0
-            )
+                die_own(partner).wait_recv()
+
             whole_values(partner)
 
         if catch > LAG:
@@ -546,7 +544,7 @@
     one = pltpu.SemaphoreType.DMA
     return pl.pallas_call(
         kernel,
-        out_shape=jax.ShapeDtypeStruct((mine, tokens, cols), BF16),
+        out_shape=pltpu.VMEM((mine, tokens, cols), BF16),
         in_specs=[hbm] * 8,
         out_specs=vmem,
         scratch_shapes=[
@@ -583,7 +581,7 @@
             pltpu.SMEM((questions,), jnp.int32),
             dma(CHUNKS + 7),
             one, dma(messages), dma(messages),
-            one, dma(CHUNKS * chips),
+            one, dma(1 + messages),
             one, one, one, dma(pieces), one, dma(mine),
             one, dma(pieces), one, dma(pieces),
             pltpu.SemaphoreType.REGULAR, pltpu.SemaphoreType.REGULAR,

time: 125 us -> 123 us (0.984)
  no operation moved by 1% of the time
where the time goes in v7:
time: 123 us
  Pallas kernels  122 us (99%)
    pallas_call x1, Pallas kernels, body(): pl.pallas_call(kernel, out_shape=pltpu.VMEM((mine, tokens, cols), BF16),...  122 us

profile of v7, /device:TPU:513, one launch (start us, length us, event | category | flops | bytes accessed | tf_op | source)
XLA Modules:
  0.0 122.7 jit_solution(9811002791449872455)
XLA Ops:
  0.0 122.0 %reader_step.1 = bf16[2,64,256]{2,1,0:T(8,128)(2,1)S(1)} custom-call(s32[8,16]{1,0:T(8,128)} %bitcast.5, bf16[128,4096]{1,0:T(8,128)(2,1)} %bitcast.3, bf16[4096]{0:T(1024)(128)(2,1)} %enc_gain_hbm.1, bf16[128,4096]{1,0:T(8,128)(2,1)} %bitcast.4, bf16[4096]{0:T(1024)(128)(2,1)} %dec_gain_hbm.1, bf16[4096,256]{1,0:T(8,128)(2,1)} %wq_hbm.1, ...), custom_call_target="tpu_custom_call" | custom-call | tf_op jit(solution)/shard_map/reader_step/pallas_call | solution.py:545
  122.1 0.6 copy.10

commit v8 on v6

--- a/solution.py
+++ b/solution.py
@@ -38,9 +38,9 @@
 
 
 def kernel(
-    table_hbm, states_hbm, enc_gain_hbm, dec_hbm, dec_gain_hbm, wq_hbm, wkv_hbm, wo_hbm, out_hbm,
+    table_hbm, states_hbm, enc_gain_hbm, dec_hbm, dec_gain_hbm, wq_hbm, wkv_hbm, wo_hbm, out_ref,
     raw, dec_raw, dec_rows, rows, wq, wkv_in, wkv, wo, kv, qbuf, num, peak, total,
-    osend, orecv, lsend, lrecv, shares, att, half, psend, precv, xsend, xrecv, out_here, gains,
+    osend, orecv, lsend, lrecv, shares, att, halves, psend, precv, xsend, xrecv, gains,
     enc_gain, dec_gain, table, first, second, hits,
     load_sem, rs, rr, lr, ds, dr, qs, qr, os_, or_, ss, sr, ps, pr, xs, xr, rising, falling,
 ):
@@ -115,9 +115,11 @@
         at = part(seq_at(x + lax.div(m, CHUNKS) + behind, c), CHUNKS - 1 - lax.rem(m, CHUNKS))
         return pltpu.make_async_remote_copy(at, at, rs, lr.at[m], device_id={"seq": left})
 
-    def die_copy(k, slot, chunk):
-        at = part(slot, chunk)
+    def die_copy(at, k):
         return pltpu.make_async_remote_copy(at, at, ds, dr.at[k], device_id={"seq": partner})
+
+    def die_own(slot):
+        return die_copy(rows.at[slot], 0)
 
     def from_left(m, core):
         return seq_at(x - lax.div(m, CHUNKS) - 1, core), lax.rem(m, CHUNKS)
@@ -146,7 +148,7 @@
 
     @pl.when(c == 0)
     def _():
-        lax.fori_loop(0, CHUNKS, lambda m, n: (die_copy(m, me, m).start(), n)[1], 0)
+        die_own(me).start()
 
     @pl.when(g == 0)
     def _():
@@ -200,20 +202,29 @@
 
     def attend(slot):
         asked = qbuf[table[g, slot]]
-        for j in range(cols // LANES):
-            at = slice(j * LANES, (j + 1) * LANES)
+        ats = [slice(j * LANES, (j + 1) * LANES) for j in range(cols // LANES)]
+        scores = []
+        for at in ats:
             pair = asked[:, at]
             none = jnp.zeros_like(pair)
             stacked = jnp.concatenate([jnp.where(low, pair, none), jnp.where(low, none, pair)], axis=0)
-            keys = kv[slot, :, at]
-            values = kv[slot, :, cols + j * LANES : cols + (j + 1) * LANES]
-            scores = lax.dot_general(
-                stacked, keys, (((1,), (1,)), ((), ())), preferred_element_type=F32
+            scores.append(
+                lax.dot_general(
+                    stacked, kv[slot, :, at], (((1,), (1,)), ((), ())), preferred_element_type=F32
+                )
             )
-            top = jnp.max(scores, axis=-1, keepdims=True)
-            weights = jnp.exp(scores - top)
-            summed = jnp.sum(weights, axis=-1, keepdims=True)
-            product = jnp.dot(weights.astype(BF16), values, preferred_element_type=F32)
+        tops = [jnp.max(one, axis=-1, keepdims=True) for one in scores]
+        weights = [jnp.exp(one - top) for one, top in zip(scores, tops)]
+        products = [
+            jnp.dot(
+                one.astype(BF16),
+                kv[slot, :, cols + j * LANES : cols + (j + 1) * LANES],
+                preferred_element_type=F32,
+            )
+            for j, one in enumerate(weights)
+        ]
+        sums = [jnp.sum(one, axis=-1, keepdims=True) for one in weights]
+        for at, top, summed, product in zip(ats, tops, sums, products):
             num[slot, :, at] = jnp.where(low, product[:tokens], product[tokens:])
             peak[slot, :, at] = jnp.where(low, top[:tokens], top[tokens:])
             total[slot, :, at] = jnp.where(low, summed[:tokens], summed[tokens:])
@@ -234,15 +245,14 @@
         kv[slot] = result.astype(BF16)
 
     def partner_part(m):
-        die_copy(CHUNKS + m, *from_left(m, other)).wait_recv()
-        die_copy(CHUNKS + messages + m, *from_right(m, other)).wait_recv()
+        die_copy(rows.at[partner, pl.ds(0, 2 * piece)], 1 + m).wait_recv()
         key_values([from_left(m, other), from_right(m, other)])
 
     def die_right(m):
-        die_copy(CHUNKS + m, *from_left(m, c)).start()
+        die_copy(part(*from_left(m, c)), 1 + m).start()
 
     def die_left(m):
-        die_copy(CHUNKS + messages + m, *from_right(m, c)).start()
+        die_copy(part(*from_right(m, c)), 1 + m).start()
 
     hold = 2
     catch = messages - 4
@@ -297,8 +307,8 @@
         def _():
             @pl.when(c == 1)
             def _():
-                die_copy(0, partner, 0).wait_recv()
-                lax.fori_loop(0, CHUNKS, lambda k, t: (die_copy(k, me, k).start(), t)[1], 0)
+                die_own(partner).wait_recv()
+                die_own(me).start()
 
                 def late(k, t):
                     die_right(k)
@@ -320,11 +330,8 @@
         def _():
             @pl.when(c == 0)
             def _():
-                die_copy(0, partner, 0).wait_recv()
-
-            lax.fori_loop(
-                1, CHUNKS, lambda k, t: (die_copy(k, partner, k).wait_recv(), t)[1], 0
-            )
+                die_own(partner).wait_recv()
+
             whole_values(partner)
 
         if catch > LAG:
@@ -495,11 +502,16 @@
             att[:size, at] = mixed.astype(BF16)
 
         attended = att[:size, :]
+        half = halves.at[p % 2]
         psend[rows_of(p), :] = jnp.dot(
             attended, wo[other], preferred_element_type=F32
         ).astype(BF16)
         pair_copy(p).start()
         half[:size, :] = jnp.dot(attended, wo[c], preferred_element_type=F32)
+
+    def spread(p):
+        own, start, size = pieces[p]
+        half = halves.at[p % 2]
         pair_copy(p).wait_recv()
 
         def add(i):
@@ -520,6 +532,11 @@
         if start == 0:
             share_of(own)
         project(p)
+        if p + 2 < len(pieces):
+            spread(p)
+        elif p + 1 == len(pieces):
+            spread(p - 1)
+            spread(p)
 
     def sent(all_of, sem):
         pltpu.make_async_remote_copy(
@@ -532,24 +549,16 @@
     sent(osend.at[:, pl.ds(0, groups - 1)], os_)
     sent(lsend.at[:, pl.ds(0, groups - 1)], ss)
     feature = pl.ds(pl.multiple_of(me * cols, cols), cols)
-    def out_store(p):
-        own, start, size = pieces[p]
-        return pltpu.make_async_copy(
-            out_here.at[rows_of(p)], out_hbm.at[own, pl.ds(start, size)], load_sem.at[p]
-        )
-
     for p in range(len(pieces)):
         at = rows_of(p)
         result = dec_raw[at, feature].astype(F32) + xsend[at, chip_part(x)].astype(F32)
         sum_all(p).wait_recv()
         for i in range(1, chips):
             result = result + xrecv[i, at].astype(F32)
-        out_here[at, :] = result.astype(BF16)
-        out_store(p).start()
+        own, start, size = pieces[p]
+        out_ref[own, start : start + size, :] = result.astype(BF16)
     sent(psend, ps)
     sent(xrecv.at[pl.ds(0, chips - 1)], xs)
-    for p in range(len(pieces)):
-        out_store(p).wait()
 
 
 def body(
@@ -568,9 +577,9 @@
     one = pltpu.SemaphoreType.DMA
     return pl.pallas_call(
         kernel,
-        out_shape=jax.ShapeDtypeStruct((mine, tokens, cols), BF16),
+        out_shape=pltpu.VMEM((mine, tokens, cols), BF16),
         in_specs=[hbm] * 8,
-        out_specs=hbm,
+        out_specs=pl.BlockSpec(memory_space=pltpu.VMEM),
         scratch_shapes=[
             pltpu.VMEM((plen, width), BF16),
             pltpu.VMEM((mine * tokens, width), BF16),
@@ -591,12 +600,11 @@
             pltpu.VMEM((mine, groups, 1, tokens * cols // HD), F32),
             pltpu.VMEM((cols // LANES, LANES, groups), F32),
             pltpu.VMEM((tokens // 2, cols), BF16),
-            pltpu.VMEM((tokens // 2, chips * cols), F32),
+            pltpu.VMEM((2, tokens // 2, chips * cols), F32),
             pltpu.VMEM((mine * tokens, chips * cols), BF16),
             pltpu.VMEM((mine * tokens, chips * cols), BF16),
             pltpu.VMEM((mine * tokens, chips * cols), BF16),
             pltpu.VMEM((chips, mine * tokens, cols), BF16),
-            pltpu.VMEM((mine * tokens, cols), BF16),
             pltpu.VMEM((16, width), F32),
             pltpu.VMEM((width,), BF16),
             pltpu.VMEM((width,), BF16),
@@ -606,7 +614,7 @@
             pltpu.SMEM((questions,), jnp.int32),
             dma(CHUNKS + 7),
             one, dma(messages), dma(messages),
-            one, dma(CHUNKS * chips),
+            one, dma(1 + messages),
             one, one, one, dma(pieces), one, dma(mine),
             one, dma(pieces), one, dma(pieces),
             pltpu.SemaphoreType.REGULAR, pltpu.SemaphoreType.REGULAR,

time: 125 us -> 123 us (0.984)
  Pallas kernels: 124 us -> 122 us
    pallas_call x1, Pallas kernels: 124 us -> 122 us  [body(): pl.pallas_call(kernel, out_shape=pltpu.VMEM((mine, tokens, cols), BF16),...]
where the time goes in v8:
time: 123 us
  Pallas kernels  122 us (99%)
    pallas_call x1, Pallas kernels, body(): pl.pallas_call(kernel, out_shape=pltpu.VMEM((mine, tokens, cols), BF16),...  122 us

profile of v8, /device:TPU:513, one launch (start us, length us, event | category | flops | bytes accessed | tf_op | source)
XLA Modules:
  0.0 122.7 jit_solution(6456113699508322982)
XLA Ops:
  0.0 122.0 %reader_step.1 = bf16[2,64,256]{2,1,0:T(8,128)(2,1)S(1)} custom-call(s32[8,16]{1,0:T(8,128)} %bitcast.5, bf16[128,4096]{1,0:T(8,128)(2,1)} %bitcast.3, bf16[4096]{0:T(1024)(128)(2,1)} %enc_gain_hbm.1, bf16[128,4096]{1,0:T(8,128)(2,1)} %bitcast.4, bf16[4096]{0:T(1024)(128)(2,1)} %dec_gain_hbm.1, bf16[4096,256]{1,0:T(8,128)(2,1)} %wq_hbm.1, ...), custom_call_target="tpu_custom_call" | custom-call | tf_op jit(solution)/shard_map/reader_step/pallas_call | solution.py:578
  122.0 0.6 copy.10

commit v9 on v7

--- a/solution.py
+++ b/solution.py
@@ -197,20 +197,29 @@
 
     def attend(slot):
         asked = qbuf[table[g, slot]]
-        for j in range(cols // LANES):
-            at = slice(j * LANES, (j + 1) * LANES)
+        ats = [slice(j * LANES, (j + 1) * LANES) for j in range(cols // LANES)]
+        scores = []
+        for at in ats:
             pair = asked[:, at]
             none = jnp.zeros_like(pair)
             stacked = jnp.concatenate([jnp.where(low, pair, none), jnp.where(low, none, pair)], axis=0)
-            keys = kv[slot, :, at]
-            values = kv[slot, :, cols + j * LANES : cols + (j + 1) * LANES]
-            scores = lax.dot_general(
-                stacked, keys, (((1,), (1,)), ((), ())), preferred_element_type=F32
+            scores.append(
+                lax.dot_general(
+                    stacked, kv[slot, :, at], (((1,), (1,)), ((), ())), preferred_element_type=F32
+                )
             )
-            top = jnp.max(scores, axis=-1, keepdims=True)
-            weights = jnp.exp(scores - top)
-            summed = jnp.sum(weights, axis=-1, keepdims=True)
-            product = jnp.dot(weights.astype(BF16), values, preferred_element_type=F32)
+        tops = [jnp.max(one, axis=-1, keepdims=True) for one in scores]
+        weights = [jnp.exp(one - top) for one, top in zip(scores, tops)]
+        products = [
+            jnp.dot(
+                one.astype(BF16),
+                kv[slot, :, cols + j * LANES : cols + (j + 1) * LANES],
+                preferred_element_type=F32,
+            )
+            for j, one in enumerate(weights)
+        ]
+        sums = [jnp.sum(one, axis=-1, keepdims=True) for one in weights]
+        for at, top, summed, product in zip(ats, tops, sums, products):
             num[slot, :, at] = jnp.where(low, product[:tokens], product[tokens:])
             peak[slot, :, at] = jnp.where(low, top[:tokens], top[tokens:])
             total[slot, :, at] = jnp.where(low, summed[:tokens], summed[tokens:])

time: 123 us -> 123 us (level)
  no operation moved by 1% of the time
where the time goes in v9:
time: 123 us; the launch traced here: 122 us
  Pallas kernels  122 us (99%)
    pallas_call x1, Pallas kernels, body(): pl.pallas_call(kernel, out_shape=pltpu.VMEM((mine, tokens, cols), BF16),...  122 us

profile of v9, /device:TPU:513, one launch (start us, length us, event | category | flops | bytes accessed | tf_op | source)
XLA Modules:
  0.0 122.5 jit_solution(12339130067228786228)
XLA Ops:
  0.0 121.9 %reader_step.1 = bf16[2,64,256]{2,1,0:T(8,128)(2,1)S(1)} custom-call(s32[8,16]{1,0:T(8,128)} %bitcast.5, bf16[128,4096]{1,0:T(8,128)(2,1)} %bitcast.3, bf16[4096]{0:T(1024)(128)(2,1)} %enc_gain_hbm.1, bf16[128,4096]{1,0:T(8,128)(2,1)} %bitcast.4, bf16[4096]{0:T(1024)(128)(2,1)} %dec_gain_hbm.1, bf16[4096,256]{1,0:T(8,128)(2,1)} %wq_hbm.1, ...), custom_call_target="tpu_custom_call" | custom-call | tf_op jit(solution)/shard_map/reader_step/pallas_call | solution.py:554
  121.9 0.6 copy.10
